TPU v7x, 16 devices: a whole 2x2x2 slice. The times are simulated.
16 devices in a mesh: dp: 4 (over z, y), tp: 4 (over x, core).
Axes of the slice: x: 2, y: 2, z: 2, core: 2. Of those that a mesh axis runs over, the one named last changes fastest.
Arguments:
- x: bfloat16 [4, 128, 2560], P('dp', 'tp'), parts along dimension 0
- ln1_gamma: float32 [2560], replicated
- ln1_beta: float32 [2560], replicated
- w_qkv: bfloat16 [2560, 32, 3, 80], P(None, 'tp')
- b_qkv: float32 [32, 3, 80], P('tp')
- w_out: bfloat16 [2560, 2560], P('tp')
- b_out: float32 [2560], replicated
- ln2_gamma: float32 [2560], replicated
- ln2_beta: float32 [2560], replicated
- w_up: bfloat16 [2560, 10240], P(None, 'tp')
- b_up: float32 [10240], P('tp')
- w_down: bfloat16 [10240, 2560], P('tp')
- b_down: float32 [2560], replicated
- grad_y: bfloat16 [4, 128, 2560], P('dp', 'tp'), parts along dimension 0
Outputs:
- output 1: bfloat16 [4, 128, 2560], P('dp', 'tp'), parts along dimension 0
- output 2: bfloat16 [4, 128, 2560], P('dp', 'tp'), parts along dimension 0
- output 3: float32 [10240], P('dp'), parts along dimension 0
- output 4: float32 [10240], P('dp'), parts along dimension 0
- output 5: bfloat16 [10240, 32, 3, 80], P('dp', 'tp'), parts along dimension 0
- output 6: float32 [128, 3, 80], P(('dp', 'tp')), parts along dimension 0
- output 7: bfloat16 [10240, 2560], P(('dp', 'tp')), parts along dimension 0
- output 8: float32 [10240], P('dp'), parts along dimension 0
- output 9: float32 [10240], P('dp'), parts along dimension 0
- output 10: float32 [10240], P('dp'), parts along dimension 0
- output 11: bfloat16 [10240, 10240], P('dp', 'tp'), parts along dimension 0
- output 12: float32 [40960], P(('dp', 'tp')), parts along dimension 0
- output 13: bfloat16 [40960, 2560], P(('dp', 'tp')), parts along dimension 0
- output 14: float32 [10240], P('dp'), parts along dimension 0
There are 4 independent parts. A program takes and returns all parts, laid end to end along the dimension named above; an argument that names none is the same for every part.
All inputs are finite; a program needn't handle non-finite values.
Results may differ from a plain program's by a relative error of at most 0.0174444.
Values are sent between devices in bfloat16 or wider.
A program may use at most 1 GiB of HBM per device.

v0:
```python
import math
import jax
import jax.numpy as jnp
from jax import lax
from jax.sharding import PartitionSpec as P

EPS = 1e-5
MASK_VALUE = -1e30


def alibi_slopes(n_heads):
    closest = 2 ** int(math.floor(math.log2(n_heads)))
    base_ratio = 2.0 ** (-8.0 / closest)
    extra_ratio = 2.0 ** (-4.0 / closest)
    remaining = min(closest, n_heads - closest)
    slopes = [base_ratio ** (i + 1) for i in range(closest)]
    slopes = slopes + [extra_ratio ** (2 * i + 1) for i in range(remaining)]
    return jnp.array(slopes, dtype=jnp.float32)


def layer_norm(values, ln_gain, ln_bias):
    row_mean = jnp.mean(values, axis=-1, keepdims=True)
    centered = values - row_mean
    variance = jnp.mean(centered * centered, axis=-1, keepdims=True)
    return centered * lax.rsqrt(variance + EPS) * ln_gain + ln_bias


def gelu_tanh(values):
    return jax.nn.gelu(values, approximate=True)


def seq_gather(values):
    return lax.all_gather(values, 'tp', axis=1, tiled=True)


def seq_reduce(values):
    return lax.psum_scatter(values, 'tp', scatter_dimension=1, tiled=True)


def solution(mesh):
    tp_size = mesh.shape['tp']

    def local_step(x, ln1_gamma, ln1_beta, w_qkv, b_qkv, w_out, b_out, ln2_gamma, ln2_beta, w_up, b_up, w_down, b_down, grad_y):
        batch_size, seq_local = x.shape[0], x.shape[1]
        local_heads, head_size = w_qkv.shape[1], w_qkv.shape[3]
        seq_full = seq_local * tp_size
        score_scale = head_size ** -0.5
        tp_index = lax.axis_index('tp')
        slopes = lax.dynamic_slice_in_dim(alibi_slopes(local_heads * tp_size), tp_index * local_heads, local_heads)
        positions = jnp.arange(seq_full)
        causal = positions[None, :] <= positions[:, None]
        alibi_bias = slopes[:, None] * positions.astype(jnp.float32)[None, :]

        x_f = x.astype(jnp.float32)
        h_full = seq_gather(layer_norm(x_f, ln1_gamma, ln1_beta).astype(jnp.bfloat16))
        qkv_vals = (jnp.einsum('bsd,dhte->bshte', h_full, w_qkv, preferred_element_type=jnp.float32) + b_qkv).astype(jnp.bfloat16)
        q_heads = qkv_vals[:, :, :, 0]
        k_heads = qkv_vals[:, :, :, 1]
        v_heads = qkv_vals[:, :, :, 2]
        scores = jnp.einsum('bihe,bjhe->bhij', q_heads, k_heads, preferred_element_type=jnp.float32) * score_scale + alibi_bias[None, :, None, :]
        prob_f = jax.nn.softmax(jnp.where(causal, scores, MASK_VALUE), axis=-1)
        prob_bf = prob_f.astype(jnp.bfloat16)
        context = jnp.einsum('bhij,bjhe->bihe', prob_bf, v_heads, preferred_element_type=jnp.float32).astype(jnp.bfloat16)
        context_flat = context.reshape(batch_size, seq_full, local_heads * head_size)
        attn_out = seq_reduce(jnp.einsum('bsc,cd->bsd', context_flat, w_out, preferred_element_type=jnp.float32).astype(jnp.bfloat16))
        x_mid = x_f + attn_out.astype(jnp.float32) + b_out
        g_full = seq_gather(layer_norm(x_mid, ln2_gamma, ln2_beta).astype(jnp.bfloat16))
        pre_act = jnp.einsum('bsd,df->bsf', g_full, w_up, preferred_element_type=jnp.float32) + b_up
        activated = gelu_tanh(pre_act).astype(jnp.bfloat16)
        mlp_out = seq_reduce(jnp.einsum('bsf,fd->bsd', activated, w_down, preferred_element_type=jnp.float32).astype(jnp.bfloat16))
        y = (x_mid + mlp_out.astype(jnp.float32) + b_down).astype(jnp.bfloat16)

        grad_y_f = grad_y.astype(jnp.float32)
        grad_b_down = lax.psum(jnp.sum(grad_y_f, axis=(0, 1)), 'tp')
        grad_m_full = seq_gather(grad_y)
        grad_w_down = jnp.einsum('bsf,bsd->fd', activated, grad_m_full, preferred_element_type=jnp.float32).astype(jnp.bfloat16)
        grad_act = jnp.einsum('bsd,fd->bsf', grad_m_full, w_down, preferred_element_type=jnp.float32).astype(jnp.bfloat16)
        _, gelu_pullback = jax.vjp(gelu_tanh, pre_act)
        grad_pre = gelu_pullback(grad_act.astype(jnp.float32))[0]
        grad_b_up = jnp.sum(grad_pre, axis=(0, 1))
        grad_pre_bf = grad_pre.astype(jnp.bfloat16)
        grad_w_up = jnp.einsum('bsd,bsf->df', g_full, grad_pre_bf, preferred_element_type=jnp.float32).astype(jnp.bfloat16)
        grad_g = seq_reduce(jnp.einsum('bsf,df->bsd', grad_pre_bf, w_up, preferred_element_type=jnp.float32).astype(jnp.bfloat16))
        _, ln2_pullback = jax.vjp(layer_norm, x_mid, ln2_gamma, ln2_beta)
        grad_mid_ln, grad_ln2_gamma, grad_ln2_beta = ln2_pullback(grad_g.astype(jnp.float32))
        grad_ln2_gamma = lax.psum(grad_ln2_gamma, 'tp')
        grad_ln2_beta = lax.psum(grad_ln2_beta, 'tp')
        grad_mid = grad_y_f + grad_mid_ln
        grad_b_out = lax.psum(jnp.sum(grad_mid, axis=(0, 1)), 'tp')
        grad_attn_full = seq_gather(grad_mid.astype(jnp.bfloat16))
        grad_w_out = jnp.einsum('bsc,bsd->cd', context_flat, grad_attn_full, preferred_element_type=jnp.float32).astype(jnp.bfloat16)
        grad_context = jnp.einsum('bsd,cd->bsc', grad_attn_full, w_out, preferred_element_type=jnp.float32).astype(jnp.bfloat16)
        grad_context = grad_context.reshape(batch_size, seq_full, local_heads, head_size)
        grad_prob = jnp.einsum('bihe,bjhe->bhij', grad_context, v_heads, preferred_element_type=jnp.float32).astype(jnp.bfloat16).astype(jnp.float32)
        grad_v = jnp.einsum('bhij,bihe->bjhe', prob_bf, grad_context, preferred_element_type=jnp.float32).astype(jnp.bfloat16)
        grad_scores = prob_f * (grad_prob - jnp.sum(grad_prob * prob_f, axis=-1, keepdims=True))
        grad_scores_bf = grad_scores.astype(jnp.bfloat16)
        grad_q = (jnp.einsum('bhij,bjhe->bihe', grad_scores_bf, k_heads, preferred_element_type=jnp.float32) * score_scale).astype(jnp.bfloat16)
        grad_k = (jnp.einsum('bhij,bihe->bjhe', grad_scores_bf, q_heads, preferred_element_type=jnp.float32) * score_scale).astype(jnp.bfloat16)
        grad_qkv = jnp.stack([grad_q, grad_k, grad_v], axis=3)
        grad_b_qkv = jnp.sum(grad_qkv, axis=(0, 1), dtype=jnp.float32)
        grad_w_qkv = jnp.einsum('bsd,bshte->dhte', h_full, grad_qkv, preferred_element_type=jnp.float32).astype(jnp.bfloat16)
        grad_h = seq_reduce(jnp.einsum('bshte,dhte->bsd', grad_qkv, w_qkv, preferred_element_type=jnp.float32).astype(jnp.bfloat16))
        _, ln1_pullback = jax.vjp(layer_norm, x_f, ln1_gamma, ln1_beta)
        grad_x_ln, grad_ln1_gamma, grad_ln1_beta = ln1_pullback(grad_h.astype(jnp.float32))
        grad_ln1_gamma = lax.psum(grad_ln1_gamma, 'tp')
        grad_ln1_beta = lax.psum(grad_ln1_beta, 'tp')
        grad_x = (grad_mid + grad_x_ln).astype(jnp.bfloat16)
        return (y, grad_x, grad_ln1_gamma, grad_ln1_beta, grad_w_qkv, grad_b_qkv, grad_w_out, grad_b_out,
                grad_ln2_gamma, grad_ln2_beta, grad_w_up, grad_b_up, grad_w_down, grad_b_down)

    row_spec = P('dp', 'tp', None)
    in_specs = (row_spec, P(), P(), P(None, 'tp', None, None), P('tp', None, None), P('tp', None), P(), P(), P(),
                P(None, 'tp'), P('tp'), P('tp', None), P(), row_spec)
    out_specs = (row_spec, row_spec, P('dp'), P('dp'), P('dp', 'tp', None, None), P(('dp', 'tp'), None, None),
                 P(('dp', 'tp'), None), P('dp'), P('dp'), P('dp'), P('dp', 'tp'), P(('dp', 'tp')), P(('dp', 'tp'), None), P('dp'))
    return jax.shard_map(local_step, mesh=mesh, in_specs=in_specs, out_specs=out_specs, check_vma=False)
```

profile of v0, /device:TPU:0, one launch (start us, length us, event | category | flops | bytes accessed | tf_op | source)
XLA Modules:
  0.0 197.8 jit_solution(10165957524569899996)
XLA Ops:
  7.3 1.2 convert_reduce_fusion.3
  8.5 1.1 fusion.45
  9.6 1.1 fusion.43
  10.7 9.6 %all_gather.12 = bf16[1,128,2560]{2,1,0:T(8,128)(2,1)} all-gather(bf16[1,32,2560]{2,1,0:T(8,128)(2,1)S(1)} %fusion.43), channel_id=1, replica_groups=mesh['dp'=4,'tp'=4] {'tp'}, dimensions={1}, use_global_device_ids=true | all-gather | bytes 819200 | tf_op jit(solution)/shard_map/all_gather | solution.py:33
  20.4 5.5 %fusion.31 = f32[128,1920]{0,1:S(1)} fusion(bf16[2560,1920]{0,1:T(8,128)(2,1)} %bitcast.116, bf16[1,128,2560]{2,1,0:T(8,128)(2,1)} %all_gather.12), kind=kOutput, calls=%fused_computation.52 | convolution fusion | flops 1258291200 | bytes 11468800
  25.9 1.1 fusion.33
  27.2 2.2 %fusion.66 = (f32[8,128]{1,0:T(8,128)S(1)}, f32[8,128,128]{1,2,0:T(8,128)}) fusion(f32[8,128]{1,0:T(8,128)S(1)} %broadcast_multiply_fusion, pred[128,128]{0,1:T(8,128)(4,1)S(1)} %iota_compare_fusion, bf16[1,128,8,3,80]{1,4,3,2,0:T(8,128)(2,1)} %fusion.33), kind=kOutput, calls=%fused_computation.122 | convolution fusion | flops 21627008 | bytes 876544 | tf_op jit(solution)/shard_map/sub | solution.py:61
  29.4 1.4 convolution_convert_fusion.9
  30.7 0.7 copy-done.14
  31.4 1.5 fusion.6
  33.0 9.0 %all_gather.14 = bf16[1,128,2560]{2,1,0:T(8,128)(2,1)} all-gather(bf16[1,32,2560]{2,1,0:T(8,128)(2,1)} %param.28), channel_id=1, replica_groups=mesh['dp'=4,'tp'=4] {'tp'}, dimensions={1}, use_global_device_ids=true | all-gather | bytes 819200 | tf_op jit(solution)/shard_map/all_gather | solution.py:33
  42.0 10.4 %reduce-scatter.5.cloned.1.call-done = bf16[1,32,2560]{2,1,0:T(8,128)(2,1)} async-done(((bf16[1,128,2560]{2,1,0:T(8,128)(2,1)}), bf16[1,32,2560]{2,1,0:T(8,128)(2,1)}) %reduce-scatter.5.cloned.1.call-update) | async-done | bytes 163856 | tf_op jit(solution)/shard_map/reduce_scatter | solution.py:37
  52.4 1.1 fusion.53
  53.5 1.1 multiply_reduce_fusion.1
  54.6 1.0 add_convert_fusion.3
  55.7 7.2 %all_gather.13 = bf16[1,128,2560]{2,1,0:T(8,128)(2,1)S(1)} all-gather(bf16[1,32,2560]{2,1,0:T(8,128)(2,1)S(1)} %add_convert_fusion.3), channel_id=1, replica_groups=mesh['dp'=4,'tp'=4] {'tp'}, dimensions={1}, use_global_device_ids=true | all-gather | bytes 819200 | tf_op jit(solution)/shard_map/all_gather | solution.py:33
  62.9 0.9 copy-done.3
  63.8 6.7 %convolution_add_fusion = f32[128,2560]{1,0:T(8,128)S(1)} fusion(bf16[2560,2560]{1,0:T(8,128)(2,1)} %param.24, bf16[1,128,2560]{2,1,0:T(8,128)(2,1)S(1)} %all_gather.13, f32[2560]{0:T(1024)S(1)} %copy-done.23), kind=kOutput, calls=%fused_computation.5 | convolution fusion | flops 1678049280 | bytes 15083520 | tf_op jit(solution)/shard_map/bsd,df->bsf/dot_general | solution.py:68
  70.4 10.4 %fusion.67 = (f32[2560]{0:T(1024)}, bf16[128,2560]{1,0:T(8,128)(2,1)S(1)}) fusion(f32[128,2560]{1,0:T(8,128)S(1)} %convolution_add_fusion, bf16[2560,2560]{1,0:T(8,128)(2,1)} %param.26, bf16[1,128,2560]{2,1,0:T(8,128)(2,1)S(1)} %copy-done.12), kind=kOutput, calls=%fused_computation.123 | convolution fusion | flops 1685255680 | bytes 15738880 | tf_op jit(solution)/shard_map/bsd,fd->bsf/dot_general | solution.py:77
  80.8 0.9 copy-done.10
  81.7 9.8 %fusion.4 = bf16[1,128,2560]{2,1,0:T(8,128)(2,1)} fusion(bf16[2560,2560]{1,0:T(8,128)(2,1)} %param.24, bf16[128,2560]{1,0:T(8,128)(2,1)S(1)} %get-tuple-element.37), kind=kOutput, calls=%fused_computation.13 | convolution fusion | flops 1678049280 | bytes 14417920 | tf_op jit(solution)/shard_map/bsf,df->bsd/dot_general | solution.py:83
  91.7 8.0 %fusion.3 = bf16[1,128,2560]{2,1,0:T(8,128)(2,1)} fusion(bf16[2560,2560]{1,0:T(8,128)(2,1)} %param.26, f32[128,2560]{1,0:T(8,128)} %copy-done.6), kind=kOutput, calls=%fused_computation.12 | convolution fusion | flops 1680998400 | bytes 15073280 | tf_op jit(solution)/shard_map/bsf,fd->bsd/dot_general | solution.py:70
  99.8 10.1 %convolution_convert_fusion = bf16[2560,2560]{1,0:T(8,128)(2,1)} fusion(bf16[1,128,2560]{2,1,0:T(8,128)(2,1)} %all_gather.14, f32[128,2560]{1,0:T(8,128)} %copy-done.6), kind=kOutput, calls=%fused_computation.1 | convolution fusion | flops 1687224320 | bytes 15073280 | tf_op jit(solution)/shard_map/bsf,bsd->fd/dot_general | solution.py:76
  109.9 1.0 reduce-scatter.9.cloned.1.call-done
  110.9 1.2 convert_reduce_fusion.2
  112.1 1.3 fusion.48
  113.5 0.5 negate_multiply_fusion.1
  114.0 18.6 %reduce-scatter.7.cloned.1.call-done = bf16[1,32,2560]{2,1,0:T(8,128)(2,1)} async-done(((bf16[1,128,2560]{2,1,0:T(8,128)(2,1)}), bf16[1,32,2560]{2,1,0:T(8,128)(2,1)}) %reduce-scatter.7.cloned.1.call-update) | async-done | bytes 163856 | tf_op jit(solution)/shard_map/reduce_scatter | solution.py:37
  132.6 2.1 %fusion.65 = (f32[2560]{0:T(1024)S(1)}, f32[1,32,2560]{2,1,0:T(8,128)S(1)}, bf16[1,32,2560]{2,1,0:T(8,128)(2,1)}, f32[2560]{0:T(1024)S(1)}) fusion(f32[32]{0:T(128)} %negate_multiply_fusion.1, f32[32]{0:T(128)S(1)} %multiply_multiply_fusion.3, f32[32]{0:T(128)S(1)} %broadcast_multiply_fusion.1, f32[2560]{0:T(1024)S(1)} %copy-done.17, ...), kind=kLoop, calls=%fused_computation.121 | loop fusion | flops 1633280 | bytes 1362432 | tf_op jit(solution)/shard_map/reduce_sum | solution.py:89
  134.6 0.7 copy-done.9
  135.4 7.4 %all_gather.15 = bf16[1,128,2560]{2,1,0:T(8,128)(2,1)S(1)} all-gather(bf16[1,32,2560]{2,1,0:T(8,128)(2,1)S(1)} %convert_element_type.190), channel_id=1, replica_groups=mesh['dp'=4,'tp'=4] {'tp'}, dimensions={1}, use_global_device_ids=true | all-gather | bytes 819200 | tf_op jit(solution)/shard_map/all_gather | solution.py:33
  142.8 0.8 copy-done.7
  143.6 1.8 convolution_convert_fusion.10
  145.4 1.1 copy.40
  146.6 1.5 multiply_reduce_fusion
  148.7 0.3 fusion.20
  149.0 6.3 %fusion.5 = bf16[1,128,2560]{2,1,0:T(8,128)(2,1)} fusion(bf16[2560,8,3,80]{0,3,2,1:T(8,128)(2,1)} %param.18, bf16[1,128,8,1,80]{1,4,2,3,0:T(8,128)(2,1)S(1)} %fusion.20, bf16[1,128,8,1,80]{1,4,2,3,0:T(8,128)(2,1)S(1)} %fusion.21, bf16[1,128,8,1,80]{1,4,2,3,0:T(8,128)(2,1)S(1)} %fusion.22), kind=kOutput, calls=%fused_computation.14 | convolution fusion | flops 1259110400 | bytes 10977280 | tf_op jit(solution)/shard_map/bshte,dhte->bsd/dot_general | solution.py:103
  155.4 6.9 %convolution_convert_fusion.1 = bf16[2560,2560]{1,0:T(8,128)(2,1)} fusion(bf16[1,128,2560]{2,1,0:T(8,128)(2,1)S(1)} %copy-done.4, bf16[128,2560]{1,0:T(8,128)(2,1)S(1)} %copy-done.11), kind=kOutput, calls=%fused_computation.2 | convolution fusion | flops 1684275200 | bytes 14417920 | tf_op jit(solution)/shard_map/bsd,bsf->df/dot_general | solution.py:82
  162.4 1.0 copy-done.5
  163.3 2.7 %fusion.29 = f32[2560,1920]{0,1:S(1)} fusion(bf16[128,1920]{0,1:T(8,128)(2,1)S(1)} %bitcast.118, bf16[1,128,2560]{2,1,0:T(8,128)(2,1)S(1)} %copy-done.5), kind=kOutput, calls=%fused_computation.50 | convolution fusion | flops 1258291200 | bytes 20807680
  166.1 4.6 %convert_element_type.208 = bf16[2560,8,3,80]{0,3,2,1:T(8,128)(2,1)} convert(f32[2560,8,3,80]{0,3,2,1:T(8,128)S(1)} %bitcast.115) | non-fusion elementwise | flops 4915200 | bytes 29491200 | tf_op jit(solution)/shard_map/convert_element_type | solution.py:102
  170.7 0.9 convert_reduce_fusion
  171.6 2.7 %convolution_convert_fusion.2 = bf16[640,2560]{1,0:T(8,128)(2,1)} fusion(bf16[128,640]{0,1:T(8,128)(2,1)S(1)} %bitcast.120, bf16[1,128,2560]{2,1,0:T(8,128)(2,1)S(1)} %copy-done.8), kind=kOutput, calls=%fused_computation.3 | convolution fusion | flops 421068800 | bytes 4096000 | tf_op jit(solution)/shard_map/bsc,bsd->cd/dot_general | solution.py:91
  174.3 0.5 reduce-scatter.11.cloned.1.call-done
  174.8 1.1 convert_reduce_fusion.1
  175.9 1.3 fusion.49
  177.2 12.1 %all-reduce = (f32[2560]{0:T(1024)}, f32[2560]{0:T(1024)}, f32[2560]{0:T(1024)}, f32[2560]{0:T(1024)}, f32[2560]{0:T(1024)}, /*index=5*/f32[2560]{0:T(1024)}) all-reduce(f32[2560]{0:T(1024)S(1)} %get-tuple-element.16, f32[2560]{0:T(1024)S(1)} %get-tuple-element.20, ...), channel_id=1, replica_groups=mesh['dp'=4,'tp'=4] {'tp'}, use_global_device_ids=true, to_apply=%region_16.17 | all-reduce | flops 15360 | bytes 122880 | tf_op jit(solution)/shard_map/psum | solution.py:106
  189.4 1.8 add_convert_fusion.1
  (70 shorter events, 1.5 us)
Async XLA Ops:
  7.2 24.2 %copy-start = (bf16[640,2560]{1,0:T(8,128)(2,1)S(1)}, bf16[640,2560]{1,0:T(8,128)(2,1)}, u32[]{:S(2)}) copy-start(bf16[640,2560]{1,0:T(8,128)(2,1)} %param.20) | copy-start | bytes 9830404
  7.2 13.1 %copy-start.21 = (f32[8,3,80]{2,0,1:T(8,128)S(1)}, f32[8,3,80]{2,0,1:T(8,128)}, u32[]{:S(2)}) copy-start(f32[8,3,80]{2,0,1:T(8,128)} %param.19) | copy-start | bytes 23044
  7.2 45.2 %reduce-scatter.5.cloned.1.call-start = ((), (), s32[]{:S(2)}) async-start(), calls=%async_computation.4 | async-start | bytes 819200 | tf_op jit(solution)/shard_map/reduce_scatter | solution.py:37
  25.9 1.1 copy-start.24
  30.7 0.7 copy-start.14
  32.9 19.5 %copy-start.2 = (bf16[1,32,2560]{2,1,0:T(8,128)(2,1)S(1)}, bf16[1,32,2560]{2,1,0:T(8,128)(2,1)}, u32[]{:S(2)}) copy-start(bf16[1,32,2560]{2,1,0:T(8,128)(2,1)} %param.15) | copy-start | bytes 491524
  32.9 19.5 %copy-start.17 = (f32[2560]{0:T(1024)S(1)}, f32[2560]{0:T(1024)}, u32[]{:S(2)}) copy-start(f32[2560]{0:T(1024)} %param.21) | copy-start | bytes 30724
  32.9 21.7 %copy-start.19 = (f32[2560]{0:T(1024)S(1)}, f32[2560]{0:T(1024)}, u32[]{:S(2)}) copy-start(f32[2560]{0:T(1024)} %param.22) | copy-start | bytes 30724
  32.9 21.7 %copy-start.22 = (f32[2560]{0:T(1024)S(1)}, f32[2560]{0:T(1024)}, u32[]{:S(2)}) copy-start(f32[2560]{0:T(1024)} %param.23) | copy-start | bytes 30724
  33.0 30.8 %copy-start.23 = (f32[2560]{0:T(1024)S(1)}, f32[2560]{0:T(1024)}, u32[]{:S(2)}) copy-start(f32[2560]{0:T(1024)} %param.25) | copy-start | bytes 30724
  33.0 77.9 %reduce-scatter.9.cloned.1.call-start = ((), (), s32[]{:S(2)}) async-start(), calls=%async_computation.6 | async-start | bytes 819200 | tf_op jit(solution)/shard_map/reduce_scatter | solution.py:37
  62.9 0.9 copy-start.3
  63.8 6.7 %copy-start.12 = (bf16[1,128,2560]{2,1,0:T(8,128)(2,1)S(1)}, bf16[1,128,2560]{2,1,0:T(8,128)(2,1)}, u32[]{:S(2)}) copy-start(bf16[1,128,2560]{2,1,0:T(8,128)(2,1)} %all_gather.14) | copy-start | bytes 1966084
  70.4 10.4 %copy-start.6 = (f32[128,2560]{1,0:T(8,128)}, f32[128,2560]{1,0:T(8,128)S(1)}, u32[]{:S(2)}) copy-start(f32[128,2560]{1,0:T(8,128)S(1)} %convolution_add_fusion) | copy-start | bytes 3932164
  80.8 0.9 copy-start.10
  91.5 41.1 %reduce-scatter.7.cloned.1.call-start = ((), (), s32[]{:S(2)}) async-start(), calls=%async_computation.5 | async-start | bytes 819200 | tf_op jit(solution)/shard_map/reduce_scatter | solution.py:37
  99.8 32.8 %copy-start.20 = (f32[2560]{0:T(1024)S(1)}, f32[2560]{0:T(1024)}, u32[]{:S(2)}) copy-start(f32[2560]{0:T(1024)} %param.27) | copy-start | bytes 30724
  99.8 75.0 %reduce-scatter.11.cloned.1.call-start = ((), (), s32[]{:S(2)}) async-start(), calls=%async_computation.7 | async-start | bytes 819200 | tf_op jit(solution)/shard_map/reduce_scatter | solution.py:37
  134.6 0.7 copy-start.9
  142.8 0.8 copy-start.7
  145.4 2.6 %copy-start.16 = (f32[8,128,128]{1,2,0:T(8,128)S(1)}, f32[8,128,128]{1,2,0:T(8,128)}, u32[]{:S(2)}) copy-start(f32[8,128,128]{1,2,0:T(8,128)} %get-tuple-element.33) | copy-start | bytes 1572868
  146.6 1.6 copy-start.13
  149.0 6.3 %copy-start.4 = (bf16[1,128,2560]{2,1,0:T(8,128)(2,1)S(1)}, bf16[1,128,2560]{2,1,0:T(8,128)(2,1)}, u32[]{:S(2)}) copy-start(bf16[1,128,2560]{2,1,0:T(8,128)(2,1)} %copy-done.3) | copy-start | bytes 1966084
  149.0 6.3 %copy-start.11 = (bf16[128,2560]{1,0:T(8,128)(2,1)S(1)}, bf16[128,2560]{1,0:T(8,128)(2,1)}, u32[]{:S(2)}) copy-start(bf16[128,2560]{1,0:T(8,128)(2,1)} %copy-done.10) | copy-start | bytes 1966084
  162.2 1.1 copy-start.5
  166.0 5.5 %copy-start.8 = (bf16[1,128,2560]{2,1,0:T(8,128)(2,1)S(1)}, bf16[1,128,2560]{2,1,0:T(8,128)(2,1)}, u32[]{:S(2)}) copy-start(bf16[1,128,2560]{2,1,0:T(8,128)(2,1)} %copy-done.7) | copy-start | bytes 1966084
  166.0 5.5 %copy-start.15 = (bf16[8,80,128]{2,1,0:T(8,128)(2,1)S(1)}, bf16[8,80,128]{2,1,0:T(8,128)(2,1)}, u32[]{:S(2)}) copy-start(bf16[8,80,128]{2,1,0:T(8,128)(2,1)} %copy-done.14) | copy-start | bytes 491524
  171.6 3.2 %copy-start.18 = (f32[2560]{0:T(1024)S(1)}, f32[2560]{0:T(1024)}, u32[]{:S(2)}) copy-start(f32[2560]{0:T(1024)} %param.16) | copy-start | bytes 30724
  171.6 19.6 %copy-start.1 = (bf16[640,2560]{1,0:T(8,128)(2,1)S(1)}, bf16[640,2560]{1,0:T(8,128)(2,1)}, u32[]{:S(2)}) copy-start(bf16[640,2560]{1,0:T(8,128)(2,1)} %param.20) | copy-start | bytes 9830404
Sparse Core Ops, SparseCore 0:
  33.1 19.2 reduce-scatter.4
  91.6 19.2 reduce-scatter.8
  114.0 18.5 reduce-scatter.6
  155.5 19.2 reduce-scatter.10
where the time goes:
time: 198 us
  matrix products  78.2 us (39%)
  blocking collectives  45.4 us (23%)
  waiting for transfers between devices  30.5 us (15%)
  other arithmetic  23 us (12%)
  between operations  14.1 us (7%)
  local copies, waits for them, and re-layouts  6.24 us (3%)
    all_gather x4, blocking collectives, seq_gather(): return lax.all_gather(values, 'tp', axis=1, tiled=True)  33.3 us
    reduce_scatter x4, waiting for transfers between devices, seq_reduce(): return lax.psum_scatter(values, 'tp', scatter_dimension=1, tiled=True)  30.4 us
    psum x1, blocking collectives, local_step(): grad_ln1_gamma = lax.psum(grad_ln1_gamma, 'tp')  12.1 us
    dot_general x1, matrix products, local_step(): jnp.einsum('bsd,fd->bsf', grad_m_full, w_down, preferred_element_type=jnp...  10.4 us
    dot_general x1, matrix products, local_step(): jnp.einsum('bsf,bsd->fd', activated, grad_m_full, preferred_element_type=...  10.1 us
    dot_general x1, matrix products, local_step(): jnp.einsum('bsf,df->bsd', grad_pre_bf, w_up, preferred_element_type=jnp.f...  9.82 us
    unnamed x2, matrix products  8.23 us
    dot_general x1, matrix products, local_step(): jnp.einsum('bsf,fd->bsd', activated, w_down, preferred_element_type=jnp.f...  7.99 us
  transfers between devices with their start and end apart: 4, of which 4 were waited for; matrix products, arithmetic and copies ran while one was open for 20% of the time, Pallas kernels for 0%

commit v1 on v0

v1 whole, which is shorter than its diff:
```python
import jax
import jax.numpy as jnp
from jax import lax
from jax.experimental import pallas as pl
from jax.experimental.pallas import tpu as pltpu
from jax.sharding import PartitionSpec as P

EPS = 1e-5
MASK_VALUE = -1e30
MESH = pl.DeviceIdType.MESH
F32 = jnp.float32
BF16 = jnp.bfloat16

D = 2560
SEQ = 128
TP = 4
ROWS = SEQ // TP
NH = 8
HD = 80
QKV = NH * 3 * HD
CTX = NH * HD
FF = 2560
AGC = 4
AGW = D // AGC
RSC = 5
RSW = D // RSC
OFF_G, OFF_ACT, OFF_QKV, OFF_O = 0, D, D + FF, D + FF + QKV
LROWS = D + FF + QKV + CTX
SLOPES = [2.0 ** (-(h + 1) / 4.0) for h in range(NH)]
NT = (((1,), (1,)), ((), ()))
NN = (((1,), (0,)), ((), ()))
TN = (((0,), (0,)), ((), ()))


def dot(a, b, dims):
    return lax.dot_general(a, b, dims, preferred_element_type=F32)


def ln_stats(v):
    mean = jnp.mean(v, axis=-1, keepdims=True)
    cen = v - mean
    var = jnp.mean(cen * cen, axis=-1, keepdims=True)
    rstd = lax.rsqrt(var + EPS)
    return cen * rstd, rstd


def ln_grad(dy, xhat, rstd, gain):
    dxh = dy * gain
    m1 = jnp.mean(dxh, axis=-1, keepdims=True)
    m2 = jnp.mean(dxh * xhat, axis=-1, keepdims=True)
    return rstd * (dxh - m1 - xhat * m2)


def block_kernel(x_hbm, gy_hbm, wq_hbm, wo_hbm, wu_hbm, wd_hbm, g1_hbm, b1_hbm, bq_hbm, bo_hbm, g2_hbm, b2_hbm, bu_hbm,
                 bd_hbm, y_hbm, gx_hbm, vec_hbm, gbu_hbm, l_hbm, r_hbm,
                 wq, wo, wu, wd, xv, gyv, g1, b1, bq, bo, g2, b2, bu, bd,
                 rbuf, lbuf, gbuf, qkvt, dqkv, ctx, dctxt, prob, act, dact, x1, dmid, outb, gbu, va, vb, vo,
                 pb, rx1, sb, rx2, wsem, lsem, osem, ssem, rsem):
    me = lax.axis_index('tp')
    ax = lax.div(me, 2)
    ak = lax.rem(me, 2)
    partner = 2 * ax + (1 - ak)
    cross = 2 * (1 - ax) + ak
    diag = 2 * (1 - ax) + (1 - ak)

    def rows(i):
        return pl.ds(pl.multiple_of(i * ROWS, ROWS), ROWS)

    sent = []
    count = {'s': 0, 'r': 0}

    def alloc(kind, n=1):
        base = count[kind]
        count[kind] += n
        return base

    def remote(src, dst, si, ri, dev):
        return pltpu.make_async_remote_copy(src_ref=src, dst_ref=dst, send_sem=ssem.at[si], recv_sem=rsem.at[ri],
                                            device_id={'tp': dev}, device_id_type=MESH)

    small = [(x_hbm, xv), (g1_hbm, g1), (b1_hbm, b1), (bq_hbm, bq), (bo_hbm, bo), (g2_hbm, g2), (b2_hbm, b2),
             (bu_hbm, bu), (bd_hbm, bd)]
    loads = [pltpu.make_async_copy(s, d, lsem.at[i]) for i, (s, d) in enumerate(small)]
    for c in loads:
        c.start()
    gm = rbuf.at[1]
    gy_full = pltpu.make_async_copy(gy_hbm, gm.at[rows(me)], lsem.at[len(small)])
    gy_full.start()
    gy_loc = pltpu.make_async_copy(gy_hbm, gyv, lsem.at[len(small) + 1])
    gy_loc.start()
    wcopies = [pltpu.make_async_copy(s, d, wsem.at[i])
               for i, (s, d) in enumerate([(wq_hbm, wq), (wo_hbm, wo), (wd_hbm, wd), (wu_hbm, wu)])]
    wcopies[0].start()
    wcopies[1].start()

    bar = pltpu.get_barrier_semaphore()
    for dev in (partner, cross, diag):
        pl.semaphore_signal(bar, inc=1, device_id={'tp': dev}, device_id_type=MESH)

    class Gather:
        def __init__(self, full):
            self.full = full
            self.s = alloc('s', 2 * AGC + 1)
            self.r = alloc('r', 2 * AGC + 1)

        def chunk(self, dev, c):
            return self.full.at[rows(dev), pl.ds(c * AGW, AGW)]

        def cross_copy(self, dev, c):
            ref = self.chunk(dev, c)
            return remote(ref, ref, self.s + c, self.r + c, cross)

        def fwd_copy(self, dev, c):
            ref = self.chunk(dev, c)
            return remote(ref, ref, self.s + AGC + c, self.r + AGC + c, partner)

        def own_copy(self, dev):
            ref = self.full.at[rows(dev)]
            return remote(ref, ref, self.s + 2 * AGC, self.r + 2 * AGC, partner)

        def start(self):
            for c in range(AGC):
                self.cross_copy(me, c).start()
            self.own_copy(me).start()

        def forward(self, c):
            self.cross_copy(cross, c).wait_recv()
            self.fwd_copy(cross, c).start()

        def finish(self):
            self.own_copy(partner).wait_recv()
            for c in range(AGC):
                self.fwd_copy(diag, c).wait_recv()

        def drain(self):
            for c in range(AGC):
                self.cross_copy(me, c).wait_send()
                self.fwd_copy(cross, c).wait_send()
            self.own_copy(me).wait_send()

    class Scatter:
        def __init__(self, i):
            self.p, self.x1, self.sb, self.x2 = pb.at[i], rx1.at[i], sb.at[i], rx2.at[i]
            self.s = alloc('s', 2 * RSC)
            self.r = alloc('r', 2 * RSC)

        def cols(self, n):
            if isinstance(n, int):
                return pl.ds(n * RSW, RSW)
            return pl.ds(pl.multiple_of(n * RSW, RSW), RSW)

        def pair(self, n):
            return remote(self.p.at[:, 1 - ak, :, self.cols(n)], self.x1.at[:, :, self.cols(n)], self.s + n, self.r + n, partner)

        def over(self, n):
            return remote(self.sb.at[:, self.cols(n)], self.x2.at[:, self.cols(n)], self.s + RSC + n, self.r + RSC + n, cross)

        def produce(self, n, val):
            self.p[:, :, :, self.cols(n)] = val.astype(BF16).reshape(2, 2, ROWS, RSW)
            self.pair(n).start()

        def relay(self, n):
            self.pair(n).wait_recv()
            self.sb[:, self.cols(n)] = (self.p[1 - ax, ak, :, self.cols(n)].astype(F32)
                                        + self.x1[1 - ax, :, self.cols(n)].astype(F32)).astype(BF16)
            self.over(n).start()

        def run(self, fn, relay=True):
            def body(n, carry):
                self.produce(n, fn(self.cols(n)))
                if relay:
                    @pl.when(n > 0)
                    def _():
                        self.relay(n - 1)
                return carry
            lax.fori_loop(0, RSC, body, 0)

        def relay_all(self):
            def body(n, carry):
                self.relay(n)
                return carry
            lax.fori_loop(0, RSC, body, 0)

        def result(self):
            for n in range(RSC):
                self.over(n).wait_recv()
            return (self.p[ax, ak].astype(F32) + self.x1[ax].astype(F32) + self.x2[...].astype(F32))

        def drain(self):
            for n in range(RSC):
                self.pair(n).wait_send()
                self.over(n).wait_send()

    gat_h, gat_m, gat_g, gat_a = Gather(rbuf.at[2]), Gather(rbuf.at[1]), Gather(gbuf), Gather(rbuf.at[3])
    sc_a, sc_g, sc_y, sc_h = Scatter(0), Scatter(1), Scatter(2), Scatter(3)
    outs = []

    def emit(src, dst):
        c = pltpu.make_async_copy(src, dst, osem.at[len(outs)])
        c.start()
        outs.append(c)

    for c in loads:
        c.wait()
    xhat1, _ = ln_stats(xv[...].astype(F32))
    rbuf[2, rows(me), :] = (xhat1 * g1[...] + b1[...]).astype(BF16)
    gy_full.wait()
    pl.semaphore_wait(bar, 3)
    gat_h.start()
    wcopies[2].start()
    wcopies[3].start()
    for c in range(AGC):
        gat_h.forward(c)
    wcopies[0].wait()
    gat_h.finish()
    gat_m.start()
    emit(rbuf.at[2], r_hbm.at[2])

    QC = 384

    def qkv_body(n, carry):
        r0 = pl.multiple_of(n * QC, QC)
        v = dot(rbuf[2], wq[pl.ds(r0, QC), :], NT) + bq[:, pl.ds(r0, QC)]
        qkvt[pl.ds(r0, QC), :] = v.astype(BF16).T
        return carry
    lax.fori_loop(0, QKV // QC, qkv_body, 0)

    scale = HD ** -0.5
    jpos = lax.broadcasted_iota(jnp.int32, (SEQ, SEQ), 0)
    ipos = lax.broadcasted_iota(jnp.int32, (SEQ, SEQ), 1)
    causal = jpos <= ipos
    jf = jpos.astype(F32)
    base = jnp.where(me == 0, 1.0, jnp.where(me == 1, 0.25, jnp.where(me == 2, 0.0625, 0.015625))).astype(F32)

    def head(h, t):
        r0 = h * 3 * HD + t * HD
        return qkvt[r0:r0 + HD, :]

    for h in range(NH):
        s = dot(head(h, 1), head(h, 0), TN) * scale + (base * SLOPES[h]) * jf
        s = jnp.where(causal, s, MASK_VALUE)
        e = jnp.exp(s - jnp.max(s, axis=0, keepdims=True))
        p = e * (1.0 / jnp.sum(e, axis=0, keepdims=True))
        prob[h] = p
        lbuf[OFF_O + h * HD:OFF_O + (h + 1) * HD, :] = dot(head(h, 2), p.astype(BF16), NN).astype(BF16)
    for t in range(CTX // 128):
        ctx[:, t * 128:(t + 1) * 128] = lbuf[OFF_O + t * 128:OFF_O + (t + 1) * 128, :].T

    wcopies[1].wait()
    sc_a.run(lambda cols: dot(ctx[...], wo[:, cols], NN))
    sc_a.relay(RSC - 1)

    for c in range(AGC):
        gat_m.forward(c)
    wcopies[2].wait()
    gat_m.finish()
    emit(rbuf.at[1], r_hbm.at[1])
    FC = 256

    def dact_body(n, carry):
        f0 = pl.multiple_of(n * FC, FC)
        dact[:, pl.ds(f0, FC)] = dot(rbuf[1], wd[pl.ds(f0, FC), :], NT).astype(BF16)
        return carry
    lax.fori_loop(0, 5, dact_body, 0)

    a = sc_a.result().astype(BF16).astype(F32)
    x1[...] = xv[...].astype(F32) + a + bo[...]
    xhat2, rstd2 = ln_stats(x1[...])
    gbuf[rows(me), :] = (xhat2 * g2[...] + b2[...]).astype(BF16)
    gat_g.start()
    lax.fori_loop(5, 10, dact_body, 0)
    for c in range(AGC):
        gat_g.forward(c)
    wcopies[3].wait()
    gat_g.finish()

    UC = 512
    k0 = 0.7978845608028654
    k1 = 0.044715

    def up_body(n, carry):
        f0 = pl.multiple_of(n * UC, UC)
        cols = pl.ds(f0, UC)
        v = dot(gbuf[...], wu[:, cols], NN) + bu[:, cols]
        v2 = v * v
        t = jnp.tanh(k0 * (v + k1 * (v2 * v)))
        hp = 0.5 * (1.0 + t)
        act[:, cols] = (v * hp).astype(BF16)
        dg = hp + (0.5 * k0) * v * (1.0 - t * t) * (1.0 + (3.0 * k1) * v2)
        dpre = dact[:, cols].astype(F32) * dg
        gbu[:, cols] = jnp.sum(dpre, axis=0, keepdims=True)
        rbuf[0, :, cols] = dpre.astype(BF16)
        return carry
    lax.fori_loop(0, FF // UC, up_body, 0)
    emit(rbuf.at[0], r_hbm.at[0])
    emit(gbu, gbu_hbm)

    def dg_chunk(cols):
        return dot(rbuf[0], wu[cols, :], NT)
    sc_g.run(dg_chunk)
    sc_g.relay(RSC - 1)

    sc_y.run(lambda cols: dot(act[...], wd[:, cols], NN), relay=False)

    def tr_body(src, off):
        def body(n, carry):
            r0 = pl.multiple_of(n * 128, 128)
            lbuf[pl.ds(off + r0, 128), :] = src[:, pl.ds(r0, 128)].T
            return carry
        return body
    lax.fori_loop(0, FF // 128, tr_body(act, OFF_ACT), 0)

    gy_loc.wait()
    dgl = sc_g.result().astype(BF16).astype(F32)
    xhat2, rstd2 = ln_stats(x1[...])
    gyf = gyv[...].astype(F32)
    dm = gyf + ln_grad(dgl, xhat2, rstd2, g2[...])
    dmid[...] = dm
    rbuf[3, rows(me), :] = dm.astype(BF16)
    gat_a.start()
    va[me, 0:1, :] = jnp.sum(dgl * xhat2, axis=0, keepdims=True)
    va[me, 1:2, :] = jnp.sum(dgl, axis=0, keepdims=True)
    va[me, 2:3, :] = jnp.sum(dm, axis=0, keepdims=True)
    va[me, 3:4, :] = jnp.sum(gyf, axis=0, keepdims=True)
    lax.fori_loop(0, D // 128, tr_body(gbuf, OFF_G), 0)
    for c in range(AGC):
        gat_a.forward(c)
    gat_a.finish()
    emit(rbuf.at[3], r_hbm.at[3])

    sva, rva = alloc('s', 3), alloc('r', 3)

    def vec_copy(buf, s, r, i, owner, dev):
        return remote(buf.at[owner], buf.at[owner], s + i, r + i, dev)
    peers = (partner, cross, diag)
    sc_y.relay_all()
    for i, dev in enumerate(peers):
        vec_copy(va, sva, rva, i, me, dev).start()

    ctx[...] = dot(rbuf[3], wo[...], NT).astype(BF16)
    for t in range(CTX // 128):
        dctxt[t * 128:(t + 1) * 128, :] = ctx[:, t * 128:(t + 1) * 128].T

    for h in range(NH):
        dot_h = dctxt[h * HD:(h + 1) * HD, :]
        p = prob[h]
        dp = dot(head(h, 2), dot_h, TN).astype(BF16).astype(F32)
        ds = (p * (dp - jnp.sum(dp * p, axis=0, keepdims=True))).astype(BF16)
        r0 = OFF_QKV + h * 3 * HD
        lbuf[r0:r0 + HD, :] = (dot(head(h, 1), ds, NN) * scale).astype(BF16)
        lbuf[r0 + HD:r0 + 2 * HD, :] = (dot(head(h, 0), ds, NT) * scale).astype(BF16)
        lbuf[r0 + 2 * HD:r0 + 3 * HD, :] = dot(dot_h, p.astype(BF16), NT).astype(BF16)
    for t in range(QKV // 128):
        dqkv[:, t * 128:(t + 1) * 128] = lbuf[OFF_QKV + t * 128:OFF_QKV + (t + 1) * 128, :].T
    emit(lbuf, l_hbm)

    sc_h.run(lambda cols: dot(dqkv[...], wq[:, cols], NN))
    sc_h.relay(RSC - 1)

    m = sc_y.result().astype(BF16).astype(F32)
    outb[0] = (x1[...] + m + bd[...]).astype(BF16)
    emit(outb.at[0], y_hbm)
    vec_copy(va, sva, rva, 0, partner, partner).wait_recv()
    vec_copy(va, sva, rva, 1, cross, cross).wait_recv()
    vec_copy(va, sva, rva, 2, diag, diag).wait_recv()
    tot = (va[0] + va[1]) + (va[2] + va[3])
    for i in range(4):
        vo[i] = tot[i:i + 1]

    dhl = sc_h.result().astype(BF16).astype(F32)
    xhat1, rstd1 = ln_stats(xv[...].astype(F32))
    vb[me, 0:1, :] = jnp.sum(dhl * xhat1, axis=0, keepdims=True)
    vb[me, 1:2, :] = jnp.sum(dhl, axis=0, keepdims=True)
    svb, rvb = alloc('s', 3), alloc('r', 3)
    for i, dev in enumerate(peers):
        vec_copy(vb, svb, rvb, i, me, dev).start()
    outb[1] = (dmid[...] + ln_grad(dhl, xhat1, rstd1, g1[...])).astype(BF16)
    emit(outb.at[1], gx_hbm)
    vec_copy(vb, svb, rvb, 0, partner, partner).wait_recv()
    vec_copy(vb, svb, rvb, 1, cross, cross).wait_recv()
    vec_copy(vb, svb, rvb, 2, diag, diag).wait_recv()
    tot = (vb[0] + vb[1]) + (vb[2] + vb[3])
    for i in range(2):
        vo[4 + i] = tot[i:i + 1]
    emit(vo, vec_hbm)

    for g in (gat_h, gat_m, gat_g, gat_a):
        g.drain()
    for s in (sc_a, sc_g, sc_y, sc_h):
        s.drain()
    for i, dev in enumerate(peers):
        vec_copy(va, sva, rva, i, me, dev).wait_send()
        vec_copy(vb, svb, rvb, i, me, dev).wait_send()
    for c in outs:
        c.wait()


GR = 320
SECTIONS = ((OFF_ACT, FF, 1), (OFF_G, D, 0), (OFF_QKV, QKV, 2), (OFF_O, CTX, 3))


def grad_kernel(y_in, gx_in, vec_in, gbu_in, l_hbm, r_hbm, y_out, gx_out, v0, v1, v2, v3, v4, v5, gbq_hbm, gbu_out,
                dwq, dwo, dwu, dwd, lv, rv, st, yv, gxv, vv, gv, gbq, isem, ssem, psem, osem):
    loads = []
    for i, (off, n, r) in enumerate(SECTIONS):
        cl = pltpu.make_async_copy(l_hbm.at[pl.ds(off, n)], lv.at[pl.ds(off, n)], isem.at[2 * i])
        cr = pltpu.make_async_copy(r_hbm.at[r], rv.at[r], isem.at[2 * i + 1])
        cl.start()
        cr.start()
        loads.append((cl, cr))
    passes = [(y_in, yv, y_out), (gx_in, gxv, gx_out), (gbu_in, gv, gbu_out)]
    pin = [pltpu.make_async_copy(a, b, psem.at[i]) for i, (a, b, _) in enumerate(passes)]
    pin.append(pltpu.make_async_copy(vec_in, vv, psem.at[3]))
    for c in pin:
        c.start()
    douts = (dwd, dwu, dwq, dwo)
    step = 0
    for i, (off, n, r) in enumerate(SECTIONS):
        loads[i][0].wait()
        loads[i][1].wait()
        dst = douts[i]

        def body(m, carry, off=off, r=r, dst=dst, step=step):
            slot = lax.rem(m + step, 3)
            out = pltpu.make_async_copy(st.at[slot], dst.at[pl.ds(pl.multiple_of(m * GR, GR), GR)], ssem.at[slot])

            @pl.when(m + step >= 3)
            def _():
                out.wait()
            st[slot] = dot(lv[pl.ds(pl.multiple_of(off + m * GR, 64), GR), :], rv[r], NN).astype(BF16)
            out.start()
            return carry
        lax.fori_loop(0, n // GR, body, 0)
        step += n // GR
    for c in pin:
        c.wait()
    done = []
    for i, (_, b, o) in enumerate(passes):
        done.append(pltpu.make_async_copy(b, o, osem.at[i]))
    for i, o in enumerate((v0, v1, v2, v3, v4, v5)):
        done.append(pltpu.make_async_copy(vv.at[i], o, osem.at[3 + i]))
    ones = jnp.ones((16, SEQ), BF16)
    for h in range(NH):
        for t in range(3):
            r0 = OFF_QKV + h * 3 * HD + t * HD
            gbq[t, h:h + 1, :] = dot(ones, lv[r0:r0 + HD, :], NT)[0:1]
    done.append(pltpu.make_async_copy(gbq, gbq_hbm, osem.at[9]))
    for c in done:
        c.start()
    for i in range(3):
        pltpu.make_async_copy(st.at[i], dwo.at[pl.ds(0, GR)], ssem.at[i]).wait()
    for c in done:
        c.wait()


def solution(mesh):
    def local_step(x, ln1_gamma, ln1_beta, w_qkv, b_qkv, w_out, b_out, ln2_gamma, ln2_beta, w_up, b_up, w_down, b_down, grad_y):
        row = lambda v: v.reshape(1, -1)
        wqt = jnp.transpose(w_qkv, (1, 2, 3, 0)).reshape(QKV, D)
        any_spec = pl.BlockSpec(memory_space=pl.ANY)
        sds = jax.ShapeDtypeStruct
        y, gx, vec, gbu, lmat, rmat = pl.pallas_call(
            block_kernel,
            name='block',
            out_shape=(sds((ROWS, D), BF16), sds((ROWS, D), BF16), sds((6, 1, D), F32), sds((1, FF), F32),
                       sds((LROWS, SEQ), BF16), sds((4, SEQ, D), BF16)),
            in_specs=[any_spec] * 14,
            out_specs=(any_spec,) * 6,
            scratch_shapes=[
                pltpu.VMEM((QKV, D), BF16), pltpu.VMEM((CTX, D), BF16), pltpu.VMEM((D, FF), BF16), pltpu.VMEM((FF, D), BF16),
                pltpu.VMEM((ROWS, D), BF16), pltpu.VMEM((ROWS, D), BF16),
                pltpu.VMEM((1, D), F32), pltpu.VMEM((1, D), F32), pltpu.VMEM((1, QKV), F32), pltpu.VMEM((1, D), F32),
                pltpu.VMEM((1, D), F32), pltpu.VMEM((1, D), F32), pltpu.VMEM((1, FF), F32), pltpu.VMEM((1, D), F32),
                pltpu.VMEM((4, SEQ, D), BF16), pltpu.VMEM((LROWS, SEQ), BF16), pltpu.VMEM((SEQ, D), BF16),
                pltpu.VMEM((QKV, SEQ), BF16), pltpu.VMEM((SEQ, QKV), BF16), pltpu.VMEM((SEQ, CTX), BF16),
                pltpu.VMEM((CTX, SEQ), BF16), pltpu.VMEM((NH, SEQ, SEQ), F32),
                pltpu.VMEM((SEQ, FF), BF16), pltpu.VMEM((SEQ, FF), BF16),
                pltpu.VMEM((ROWS, D), F32), pltpu.VMEM((ROWS, D), F32), pltpu.VMEM((2, ROWS, D), BF16),
                pltpu.VMEM((1, FF), F32),
                pltpu.VMEM((TP, 4, D), F32), pltpu.VMEM((TP, 2, D), F32), pltpu.VMEM((6, 1, D), F32),
                pltpu.VMEM((4, 2, 2, ROWS, D), BF16), pltpu.VMEM((4, 2, ROWS, D), BF16),
                pltpu.VMEM((4, ROWS, D), BF16), pltpu.VMEM((4, ROWS, D), BF16),
                pltpu.SemaphoreType.DMA((4,)), pltpu.SemaphoreType.DMA((11,)), pltpu.SemaphoreType.DMA((10,)),
                pltpu.SemaphoreType.DMA((82,)), pltpu.SemaphoreType.DMA((82,)),
            ],
            compiler_params=pltpu.CompilerParams(collective_id=0, has_side_effects=True, vmem_limit_bytes=66_000_000),
            cost_estimate=pl.CostEstimate(flops=10_000_000_000, bytes_accessed=45_000_000, transcendentals=1_000_000),
        )(x[0], grad_y[0], wqt, w_out, w_up, w_down, row(ln1_gamma), row(ln1_beta), b_qkv.reshape(1, QKV), row(b_out),
          row(ln2_gamma), row(ln2_beta), row(b_up), row(b_down))
        y, gx, v0, v1, v2, v3, v4, v5, gbq, gbu, dwq, dwo, dwu, dwd = pl.pallas_call(
            grad_kernel,
            name='weight_grads',
            out_shape=(sds((ROWS, D), BF16), sds((ROWS, D), BF16)) + (sds((1, D), F32),) * 6 + (
                sds((3, NH, HD), F32), sds((1, FF), F32), sds((QKV, D), BF16), sds((CTX, D), BF16), sds((D, FF), BF16), sds((FF, D), BF16)),
            in_specs=[any_spec] * 6,
            out_specs=(any_spec,) * 14,
            scratch_shapes=[
                pltpu.VMEM((LROWS, SEQ), BF16), pltpu.VMEM((4, SEQ, D), BF16), pltpu.VMEM((3, GR, D), BF16),
                pltpu.VMEM((ROWS, D), BF16), pltpu.VMEM((ROWS, D), BF16), pltpu.VMEM((6, 1, D), F32), pltpu.VMEM((1, FF), F32),
                pltpu.VMEM((3, NH, HD), F32),
                pltpu.SemaphoreType.DMA((8,)), pltpu.SemaphoreType.DMA((3,)), pltpu.SemaphoreType.DMA((4,)), pltpu.SemaphoreType.DMA((10,)),
            ],
            compiler_params=pltpu.CompilerParams(vmem_limit_bytes=40_000_000),
            cost_estimate=pl.CostEstimate(flops=5_000_000_000, bytes_accessed=44_000_000, transcendentals=0),
        )(y, gx, vec, gbu, lmat, rmat)
        g_wqkv = jnp.transpose(dwq.reshape(NH, 3, HD, D), (3, 0, 1, 2))
        vecs = [v.reshape(D) for v in (v0, v1, v2, v3, v4, v5)]
        g_ln2g, g_ln2b, g_bo, g_bd, g_ln1g, g_ln1b = vecs
        return (y[None], gx[None], g_ln1g, g_ln1b, g_wqkv, jnp.transpose(gbq, (1, 0, 2)), dwo, g_bo,
                g_ln2g, g_ln2b, dwu, gbu.reshape(FF), dwd, g_bd)

    row_spec = P('dp', 'tp', None)
    in_specs = (row_spec, P(), P(), P(None, 'tp', None, None), P('tp', None, None), P('tp', None), P(), P(), P(),
                P(None, 'tp'), P('tp'), P('tp', None), P(), row_spec)
    out_specs = (row_spec, row_spec, P('dp'), P('dp'), P('dp', 'tp', None, None), P(('dp', 'tp'), None, None),
                 P(('dp', 'tp'), None), P('dp'), P('dp'), P('dp'), P('dp', 'tp'), P(('dp', 'tp')), P(('dp', 'tp'), None), P('dp'))
    return jax.shard_map(local_step, mesh=mesh, in_specs=in_specs, out_specs=out_specs, check_vma=False)
```

time: 198 us -> 110 us (0.56)
  Pallas kernels: 0 us -> 86.6 us
  matrix products: 78.2 us -> 0 us
  blocking collectives: 45.4 us -> 0 us
  waiting for transfers between devices: 30.5 us -> 0 us
  other arithmetic: 23 us -> 4.39 us
  between operations: 14.1 us -> 0.68 us
  local copies, waits for them, and re-layouts: 6.24 us -> 17.2 us
    pallas_call x0 -> x2, Pallas kernels: none -> 86.6 us  [the longest x1 68.9 us: local_step(): pl.pallas_call(block_kernel, name='block', out_shape=(sds((ROWS, D), BF16...]
    dot_general x15 -> x0, matrix products: 67.8 us -> none  [the longest x1 10.4 us: local_step(): jnp.einsum('bsd,fd->bsf', grad_m_full, w_down, preferred_element_type=jnp...]
    all_gather x4 -> x0, blocking collectives: 33.3 us -> none  [seq_gather(): return lax.all_gather(values, 'tp', axis=1, tiled=True)]
    reduce_scatter x4 -> x0, waiting for transfers between devices: 30.4 us -> none  [seq_reduce(): return lax.psum_scatter(values, 'tp', scatter_dimension=1, tiled=True)]
    reduce_sum x10 -> x0, other arithmetic: 12.5 us -> none  [the longest x4 5.02 us: layer_norm(): return centered * lax.rsqrt(variance + EPS) * ln_gain + ln_bias]
    psum x1 -> x0, blocking collectives: 12.1 us -> none  [local_step(): grad_ln1_gamma = lax.psum(grad_ln1_gamma, 'tp')]
    reshape x0 -> x8, local copies, waits for them, and re-layouts: none -> 9.87 us  [the longest x7 9.19 us: local_step(): row = lambda v: v.reshape(1, -1)]
    convert_element_type x8 -> x0, other arithmetic: 9.79 us -> none  [the longest x1 4.64 us: local_step(): jnp.einsum('bsd,bshte->dhte', h_full, grad_qkv, preferred_element_type=jn...]
  transfers between devices with their start and end apart: 4 -> 0, of which waited for: 4 -> 0; matrix products, arithmetic and copies ran while one was open for 20% -> 0% of each run, Pallas kernels for 0% -> 0%
where the time goes in v1:
time: 110 us; the launch traced here: 109 us
  Pallas kernels  86.6 us (79%)
  local copies, waits for them, and re-layouts  17.2 us (16%)
  other arithmetic  4.39 us (4%)
    pallas_call x1, Pallas kernels, local_step(): pl.pallas_call(block_kernel, name='block', out_shape=(sds((ROWS, D), BF16...  68.9 us
    pallas_call x1, Pallas kernels, local_step(): pl.pallas_call(grad_kernel, name='weight_grads', out_shape=(sds((ROWS, D)...  17.7 us
    reshape x7, local copies, waits for them, and re-layouts, local_step(): row = lambda v: v.reshape(1, -1)  9.19 us
    unnamed x13, local copies, waits for them, and re-layouts  7.35 us
    pallas_call x7, other arithmetic, local_step(): pl.pallas_call(grad_kernel, name='weight_grads', out_shape=(sds((ROWS, D)...  4.39 us

profile of v1, /device:TPU:0, one launch (start us, length us, event | category | flops | bytes accessed | tf_op | source)
XLA Modules:
  0.0 108.9 jit_solution(8073486594143088108)
XLA Ops:
  0.6 1.3 %reshape.80.g1_hbm = f32[1,2560]{1,0:T(1,128)} reshape(f32[2560]{0:T(1024)} %param.15) | data formatting | bytes 20480 | tf_op jit(solution)/shard_map/reshape | solution.py:458
  2.0 1.3 %reshape.81.b1_hbm = f32[1,2560]{1,0:T(1,128)} reshape(f32[2560]{0:T(1024)} %param.16) | data formatting | bytes 20480 | tf_op jit(solution)/shard_map/reshape | solution.py:458
  3.3 1.3 %reshape.83.bo_hbm = f32[1,2560]{1,0:T(1,128)} reshape(f32[2560]{0:T(1024)} %param.20) | data formatting | bytes 20480 | tf_op jit(solution)/shard_map/reshape | solution.py:458
  4.6 1.3 %reshape.84.g2_hbm = f32[1,2560]{1,0:T(1,128)} reshape(f32[2560]{0:T(1024)} %param.21) | data formatting | bytes 20480 | tf_op jit(solution)/shard_map/reshape | solution.py:458
  5.9 1.3 %reshape.85.b2_hbm = f32[1,2560]{1,0:T(1,128)} reshape(f32[2560]{0:T(1024)} %param.22) | data formatting | bytes 20480 | tf_op jit(solution)/shard_map/reshape | solution.py:458
  7.2 1.3 %reshape.86.bu_hbm = f32[1,2560]{1,0:T(1,128)} reshape(f32[2560]{0:T(1024)} %param.24) | data formatting | bytes 20480 | tf_op jit(solution)/shard_map/reshape | solution.py:458
  8.5 1.3 %reshape.87.bd_hbm = f32[1,2560]{1,0:T(1,128)} reshape(f32[2560]{0:T(1024)} %param.26) | data formatting | bytes 20480 | tf_op jit(solution)/shard_map/reshape | solution.py:458
  9.8 0.7 copy.29
  10.5 0.7 reshape.82.bq_hbm
  11.2 68.9 %block.1 = (bf16[32,2560]{1,0:T(8,128)(2,1)}, bf16[32,2560]{1,0:T(8,128)(2,1)}, f32[6,1,2560]{2,1,0:T(1,128)}, f32[1,2560]{1,0:T(1,128)}, bf16[7680,128]{1,0:T(8,128)(2,1)}, /*index=5*/bf16[4,128,2560]{2,1,0:T(8,128)(2,1)}) custom-call(bf16[32,2560]{1,0:T(8,128)(2,1)} %bitcast.12, bf16[32,2560]{1,0:T(8,128)(2,1)} %bitcast.13, bf16[1920,2560]{1,0:T(8,128)(2,1)} %bitcast.11, ...), custom_call_target="tpu_custom_call" | custom-call | flops 10000000000 | bytes 45000000 | tf_op jit(solution)/shard_map/block/pallas_call | solution.py:462
  80.1 0.0 copy-start
  80.1 1.7 %copy-done = bf16[4,128,2560]{2,1,0:T(8,128)(2,1)S(1)} copy-done((bf16[4,128,2560]{2,1,0:T(8,128)(2,1)S(1)}, bf16[4,128,2560]{2,1,0:T(8,128)(2,1)}, u32[]{:S(2)}) %copy-start) | copy-done | bytes 2621464
  81.9 0.0 copy-start.1
  81.9 1.5 %copy-done.1 = bf16[7680,128]{1,0:T(8,128)(2,1)S(1)} copy-done((bf16[7680,128]{1,0:T(8,128)(2,1)S(1)}, bf16[7680,128]{1,0:T(8,128)(2,1)}, u32[]{:S(2)}) %copy-start.1) | copy-done | bytes 1966104
  83.4 0.0 copy-start.2
  83.4 0.9 copy-done.2
  84.3 0.0 copy-start.3
  84.3 0.9 copy-done.3
  85.3 0.0 copy-start.4
  85.3 0.8 copy-done.4
  86.1 0.0 copy-start.5
  86.1 0.7 copy-done.5
  86.8 17.7 %weight_grads.1 = (bf16[32,2560]{1,0:T(8,128)(2,1)}, bf16[32,2560]{1,0:T(8,128)(2,1)}, f32[1,2560]{1,0:T(1,128)S(1)}, f32[1,2560]{1,0:T(1,128)S(1)}, f32[1,2560]...) custom-call(bf16[32,2560]{1,0:T(8,128)(2,1)S(1)} %copy-done.2, ...), custom_call_target="tpu_custom_call" | custom-call | flops 5000000000 | bytes 44000000 | tf_op jit(solution)/shard_map/weight_grads/pallas_call | solution.py:490
  104.5 0.6 reduce
  105.1 0.6 reduce.1
  105.7 0.6 reduce.2
  106.4 0.6 reduce.3
  107.0 0.6 reduce.4
  107.6 0.6 reduce.5
  108.3 0.6 reduce.6
Async XLA Ops:
  80.1 1.7 %copy-start = (bf16[4,128,2560]{2,1,0:T(8,128)(2,1)S(1)}, bf16[4,128,2560]{2,1,0:T(8,128)(2,1)}, u32[]{:S(2)}) copy-start(bf16[4,128,2560]{2,1,0:T(8,128)(2,1)} %get-tuple-element.39.r_hbm) | copy-start | bytes 7864324
  81.9 1.5 %copy-start.1 = (bf16[7680,128]{1,0:T(8,128)(2,1)S(1)}, bf16[7680,128]{1,0:T(8,128)(2,1)}, u32[]{:S(2)}) copy-start(bf16[7680,128]{1,0:T(8,128)(2,1)} %get-tuple-element.38.l_hbm) | copy-start | bytes 5898244
  83.4 0.9 copy-start.2
  84.3 0.9 copy-start.3
  85.3 0.8 copy-start.4
  86.1 0.7 copy-start.5

commit v2 on v1

--- a/solution.py
+++ b/solution.py
@@ -21,6 +21,7 @@
 CTX = NH * HD
 FF = 2560
 AGC = 4
+NSEM = 64
 AGW = D // AGC
 RSC = 5
 RSW = D // RSC
@@ -53,7 +54,7 @@
 
 def block_kernel(x_hbm, gy_hbm, wq_hbm, wo_hbm, wu_hbm, wd_hbm, g1_hbm, b1_hbm, bq_hbm, bo_hbm, g2_hbm, b2_hbm, bu_hbm,
                  bd_hbm, y_hbm, gx_hbm, vec_hbm, gbu_hbm, l_hbm, r_hbm,
-                 wq, wo, wu, wd, xv, gyv, g1, b1, bq, bo, g2, b2, bu, bd,
+                 wq, wo, wu, wd, xh, g1, b1, bqv, bq, bo, g2, b2, bu, bd,
                  rbuf, lbuf, gbuf, qkvt, dqkv, ctx, dctxt, prob, act, dact, x1, dmid, outb, gbu, va, vb, vo,
                  pb, rx1, sb, rx2, wsem, lsem, osem, ssem, rsem):
     me = lax.axis_index('tp')
@@ -62,11 +63,14 @@
     partner = 2 * ax + (1 - ak)
     cross = 2 * (1 - ax) + ak
     diag = 2 * (1 - ax) + (1 - ak)
+    peers = (partner, cross, diag)
 
     def rows(i):
         return pl.ds(pl.multiple_of(i * ROWS, ROWS), ROWS)
 
-    sent = []
+    def block_rows(b):
+        return rows(2 * b + ak)
+
     count = {'s': 0, 'r': 0}
 
     def alloc(kind, n=1):
@@ -78,24 +82,23 @@
         return pltpu.make_async_remote_copy(src_ref=src, dst_ref=dst, send_sem=ssem.at[si], recv_sem=rsem.at[ri],
                                             device_id={'tp': dev}, device_id_type=MESH)
 
-    small = [(x_hbm, xv), (g1_hbm, g1), (b1_hbm, b1), (bq_hbm, bq), (bo_hbm, bo), (g2_hbm, g2), (b2_hbm, b2),
-             (bu_hbm, bu), (bd_hbm, bd)]
-    loads = [pltpu.make_async_copy(s, d, lsem.at[i]) for i, (s, d) in enumerate(small)]
+    x_load = pltpu.make_async_copy(x_hbm, xh.at[ax], lsem.at[0])
+    x_load.start()
+    small = [(g1_hbm, g1.at[0]), (b1_hbm, b1.at[0]), (bq_hbm, bqv), (bo_hbm, bo.at[0]), (g2_hbm, g2.at[0]), (b2_hbm, b2.at[0]),
+             (bu_hbm, bu.at[0]), (bd_hbm, bd.at[0])]
+    loads = [pltpu.make_async_copy(s, d, lsem.at[1 + i]) for i, (s, d) in enumerate(small)]
     for c in loads:
         c.start()
-    gm = rbuf.at[1]
-    gy_full = pltpu.make_async_copy(gy_hbm, gm.at[rows(me)], lsem.at[len(small)])
-    gy_full.start()
-    gy_loc = pltpu.make_async_copy(gy_hbm, gyv, lsem.at[len(small) + 1])
-    gy_loc.start()
+    gy_load = pltpu.make_async_copy(gy_hbm, rbuf.at[1, rows(me)], lsem.at[1 + len(small)])
+    gy_load.start()
     wcopies = [pltpu.make_async_copy(s, d, wsem.at[i])
                for i, (s, d) in enumerate([(wq_hbm, wq), (wo_hbm, wo), (wd_hbm, wd), (wu_hbm, wu)])]
+
+    bar = pltpu.get_barrier_semaphore()
+    for dev in peers:
+        pl.semaphore_signal(bar, inc=1, device_id={'tp': dev}, device_id_type=MESH)
     wcopies[0].start()
     wcopies[1].start()
-
-    bar = pltpu.get_barrier_semaphore()
-    for dev in (partner, cross, diag):
-        pl.semaphore_signal(bar, inc=1, device_id={'tp': dev}, device_id_type=MESH)
 
     class Gather:
         def __init__(self, full):
@@ -138,9 +141,30 @@
                 self.fwd_copy(cross, c).wait_send()
             self.own_copy(me).wait_send()
 
-    class Scatter:
-        def __init__(self, i):
+    class Share:
+        def __init__(self, full):
+            self.full = full
+            self.s = alloc('s', 2)
+            self.r = alloc('r', 2)
+
+        def copy(self, b, k, i):
+            ref = self.full.at[rows(2 * b + k)]
+            return remote(ref, ref, self.s + i, self.r + i, partner)
+
+        def send(self, b, i):
+            self.copy(b, ak, i).start()
+
+        def finish(self, b, i):
+            self.copy(b, 1 - ak, i).wait_recv()
+
+        def drain(self):
+            self.copy(ax, ak, 0).wait_send()
+            self.copy(1 - ax, ak, 1).wait_send()
+
+    class Reduce:
+        def __init__(self, i, both):
             self.p, self.x1, self.sb, self.x2 = pb.at[i], rx1.at[i], sb.at[i], rx2.at[i]
+            self.both = both
             self.s = alloc('s', 2 * RSC)
             self.r = alloc('r', 2 * RSC)
 
@@ -153,7 +177,11 @@
             return remote(self.p.at[:, 1 - ak, :, self.cols(n)], self.x1.at[:, :, self.cols(n)], self.s + n, self.r + n, partner)
 
         def over(self, n):
-            return remote(self.sb.at[:, self.cols(n)], self.x2.at[:, self.cols(n)], self.s + RSC + n, self.r + RSC + n, cross)
+            if self.both:
+                src, dst = self.sb.at[:, :, self.cols(n)], self.x2.at[:, :, self.cols(n)]
+            else:
+                src, dst = self.sb.at[0, :, self.cols(n)], self.x2.at[0, :, self.cols(n)]
+            return remote(src, dst, self.s + RSC + n, self.r + RSC + n, cross)
 
         def produce(self, n, val):
             self.p[:, :, :, self.cols(n)] = val.astype(BF16).reshape(2, 2, ROWS, RSW)
@@ -161,8 +189,11 @@
 
         def relay(self, n):
             self.pair(n).wait_recv()
-            self.sb[:, self.cols(n)] = (self.p[1 - ax, ak, :, self.cols(n)].astype(F32)
-                                        + self.x1[1 - ax, :, self.cols(n)].astype(F32)).astype(BF16)
+            c = self.cols(n)
+            if self.both:
+                self.sb[:, :, c] = (self.p[:, ak, :, c].astype(F32) + self.x1[:, :, c].astype(F32)).astype(BF16)
+            else:
+                self.sb[0, :, c] = (self.p[1 - ax, ak, :, c].astype(F32) + self.x1[1 - ax, :, c].astype(F32)).astype(BF16)
             self.over(n).start()
 
         def run(self, fn, relay=True):
@@ -174,6 +205,8 @@
                         self.relay(n - 1)
                 return carry
             lax.fori_loop(0, RSC, body, 0)
+            if relay:
+                self.relay(RSC - 1)
 
         def relay_all(self):
             def body(n, carry):
@@ -181,18 +214,26 @@
                 return carry
             lax.fori_loop(0, RSC, body, 0)
 
-        def result(self):
+        def arrive(self):
             for n in range(RSC):
                 self.over(n).wait_recv()
-            return (self.p[ax, ak].astype(F32) + self.x1[ax].astype(F32) + self.x2[...].astype(F32))
+
+        def block(self, b):
+            return (self.sb[b].astype(F32) + self.x2[b].astype(F32)).astype(BF16).astype(F32)
+
+        def own(self):
+            v = self.p[ax, ak].astype(F32) + self.x1[ax].astype(F32) + self.x2[0].astype(F32)
+            return v.astype(BF16).astype(F32)
 
         def drain(self):
             for n in range(RSC):
                 self.pair(n).wait_send()
                 self.over(n).wait_send()
 
-    gat_h, gat_m, gat_g, gat_a = Gather(rbuf.at[2]), Gather(rbuf.at[1]), Gather(gbuf), Gather(rbuf.at[3])
-    sc_a, sc_g, sc_y, sc_h = Scatter(0), Scatter(1), Scatter(2), Scatter(3)
+    gat_m = Gather(rbuf.at[1])
+    sh_h, sh_g, sh_a = Share(rbuf.at[2]), Share(gbuf), Share(rbuf.at[3])
+    sc_a, sc_g, sc_y, sc_h = Reduce(0, True), Reduce(1, True), Reduce(2, False), Reduce(3, False)
+    blocks = ((ax, 0), (1 - ax, 1))
     outs = []
 
     def emit(src, dst):
@@ -200,20 +241,26 @@
         c.start()
         outs.append(c)
 
+    sx, rx = alloc('s'), alloc('r')
+    x_load.wait()
+    pl.semaphore_wait(bar, 3)
+    remote(xh.at[ax], xh.at[ax], sx, rx, cross).start()
     for c in loads:
         c.wait()
-    xhat1, _ = ln_stats(xv[...].astype(F32))
-    rbuf[2, rows(me), :] = (xhat1 * g1[...] + b1[...]).astype(BF16)
-    gy_full.wait()
-    pl.semaphore_wait(bar, 3)
-    gat_h.start()
+    bq[...] = jnp.concatenate([bqv[t, h:h + 1, :] for h in range(NH) for t in range(3)], axis=1)
+    for b, i in blocks:
+        if i == 1:
+            remote(xh.at[1 - ax], xh.at[1 - ax], sx, rx, cross).wait_recv()
+        xhat, _ = ln_stats(xh[b].astype(F32))
+        rbuf[2, block_rows(b), :] = (xhat * g1[...] + b1[...]).astype(BF16)
+        sh_h.send(b, i)
+    gy_load.wait()
+    gat_m.start()
     wcopies[2].start()
     wcopies[3].start()
-    for c in range(AGC):
-        gat_h.forward(c)
     wcopies[0].wait()
-    gat_h.finish()
-    gat_m.start()
+    for b, i in blocks:
+        sh_h.finish(b, i)
     emit(rbuf.at[2], r_hbm.at[2])
 
     QC = 384
@@ -248,7 +295,6 @@
 
     wcopies[1].wait()
     sc_a.run(lambda cols: dot(ctx[...], wo[:, cols], NN))
-    sc_a.relay(RSC - 1)
 
     for c in range(AGC):
         gat_m.forward(c)
@@ -261,18 +307,17 @@
         f0 = pl.multiple_of(n * FC, FC)
         dact[:, pl.ds(f0, FC)] = dot(rbuf[1], wd[pl.ds(f0, FC), :], NT).astype(BF16)
         return carry
-    lax.fori_loop(0, 5, dact_body, 0)
-
-    a = sc_a.result().astype(BF16).astype(F32)
-    x1[...] = xv[...].astype(F32) + a + bo[...]
-    xhat2, rstd2 = ln_stats(x1[...])
-    gbuf[rows(me), :] = (xhat2 * g2[...] + b2[...]).astype(BF16)
-    gat_g.start()
-    lax.fori_loop(5, 10, dact_body, 0)
-    for c in range(AGC):
-        gat_g.forward(c)
+    lax.fori_loop(0, FF // FC, dact_body, 0)
+
+    sc_a.arrive()
+    for b, i in blocks:
+        x1[b] = xh[b].astype(F32) + sc_a.block(b) + bo[...]
+        xhat, _ = ln_stats(x1[b])
+        gbuf[block_rows(b), :] = (xhat * g2[...] + b2[...]).astype(BF16)
+        sh_g.send(b, i)
     wcopies[3].wait()
-    gat_g.finish()
+    for b, i in blocks:
+        sh_g.finish(b, i)
 
     UC = 512
     k0 = 0.7978845608028654
@@ -298,9 +343,8 @@
     def dg_chunk(cols):
         return dot(rbuf[0], wu[cols, :], NT)
     sc_g.run(dg_chunk)
-    sc_g.relay(RSC - 1)
-
-    sc_y.run(lambda cols: dot(act[...], wd[:, cols], NN), relay=False)
+
+    sc_y.run(lambda cols: dot(act[...], wd[:, cols], NN))
 
     def tr_body(src, off):
         def body(n, carry):
@@ -309,33 +353,33 @@
             return carry
         return body
     lax.fori_loop(0, FF // 128, tr_body(act, OFF_ACT), 0)
-
-    gy_loc.wait()
-    dgl = sc_g.result().astype(BF16).astype(F32)
-    xhat2, rstd2 = ln_stats(x1[...])
-    gyf = gyv[...].astype(F32)
-    dm = gyf + ln_grad(dgl, xhat2, rstd2, g2[...])
-    dmid[...] = dm
-    rbuf[3, rows(me), :] = dm.astype(BF16)
-    gat_a.start()
-    va[me, 0:1, :] = jnp.sum(dgl * xhat2, axis=0, keepdims=True)
+    lax.fori_loop(0, D // 128, tr_body(gbuf, OFF_G), 0)
+    va[me, 3:4, :] = jnp.sum(rbuf[1, rows(me), :].astype(F32), axis=0, keepdims=True)
+
+    sc_g.arrive()
+    for b, i in blocks:
+        dgl = sc_g.block(b)
+        xhat, rstd = ln_stats(x1[b])
+        dm = rbuf[1, block_rows(b), :].astype(F32) + ln_grad(dgl, xhat, rstd, g2[...])
+        rbuf[3, block_rows(b), :] = dm.astype(BF16)
+        sh_a.send(b, i)
+        if i == 0:
+            dmid[...] = dm
+    va[me, 2:3, :] = jnp.sum(dmid[...], axis=0, keepdims=True)
+    dgl = sc_g.block(ax)
+    xhat, _ = ln_stats(x1[ax])
+    va[me, 0:1, :] = jnp.sum(dgl * xhat, axis=0, keepdims=True)
     va[me, 1:2, :] = jnp.sum(dgl, axis=0, keepdims=True)
-    va[me, 2:3, :] = jnp.sum(dm, axis=0, keepdims=True)
-    va[me, 3:4, :] = jnp.sum(gyf, axis=0, keepdims=True)
-    lax.fori_loop(0, D // 128, tr_body(gbuf, OFF_G), 0)
-    for c in range(AGC):
-        gat_a.forward(c)
-    gat_a.finish()
-    emit(rbuf.at[3], r_hbm.at[3])
 
     sva, rva = alloc('s', 3), alloc('r', 3)
 
     def vec_copy(buf, s, r, i, owner, dev):
         return remote(buf.at[owner], buf.at[owner], s + i, r + i, dev)
-    peers = (partner, cross, diag)
-    sc_y.relay_all()
     for i, dev in enumerate(peers):
         vec_copy(va, sva, rva, i, me, dev).start()
+    for b, i in blocks:
+        sh_a.finish(b, i)
+    emit(rbuf.at[3], r_hbm.at[3])
 
     ctx[...] = dot(rbuf[3], wo[...], NT).astype(BF16)
     for t in range(CTX // 128):
@@ -355,20 +399,19 @@
     emit(lbuf, l_hbm)
 
     sc_h.run(lambda cols: dot(dqkv[...], wq[:, cols], NN))
-    sc_h.relay(RSC - 1)
-
-    m = sc_y.result().astype(BF16).astype(F32)
-    outb[0] = (x1[...] + m + bd[...]).astype(BF16)
+
+    sc_y.arrive()
+    outb[0] = (x1[ax] + sc_y.own() + bd[...]).astype(BF16)
     emit(outb.at[0], y_hbm)
-    vec_copy(va, sva, rva, 0, partner, partner).wait_recv()
-    vec_copy(va, sva, rva, 1, cross, cross).wait_recv()
-    vec_copy(va, sva, rva, 2, diag, diag).wait_recv()
+    for i, dev in enumerate(peers):
+        vec_copy(va, sva, rva, i, dev, dev).wait_recv()
     tot = (va[0] + va[1]) + (va[2] + va[3])
     for i in range(4):
         vo[i] = tot[i:i + 1]
 
-    dhl = sc_h.result().astype(BF16).astype(F32)
-    xhat1, rstd1 = ln_stats(xv[...].astype(F32))
+    sc_h.arrive()
+    dhl = sc_h.own()
+    xhat1, rstd1 = ln_stats(xh[ax].astype(F32))
     vb[me, 0:1, :] = jnp.sum(dhl * xhat1, axis=0, keepdims=True)
     vb[me, 1:2, :] = jnp.sum(dhl, axis=0, keepdims=True)
     svb, rvb = alloc('s', 3), alloc('r', 3)
@@ -376,23 +419,23 @@
         vec_copy(vb, svb, rvb, i, me, dev).start()
     outb[1] = (dmid[...] + ln_grad(dhl, xhat1, rstd1, g1[...])).astype(BF16)
     emit(outb.at[1], gx_hbm)
-    vec_copy(vb, svb, rvb, 0, partner, partner).wait_recv()
-    vec_copy(vb, svb, rvb, 1, cross, cross).wait_recv()
-    vec_copy(vb, svb, rvb, 2, diag, diag).wait_recv()
+    remote(xh.at[ax], xh.at[ax], sx, rx, cross).wait_send()
+    gat_m.drain()
+    for g in (sh_h, sh_g, sh_a, sc_a, sc_g, sc_y, sc_h):
+        g.drain()
+    for i, dev in enumerate(peers):
+        vec_copy(va, sva, rva, i, me, dev).wait_send()
+    for i, dev in enumerate(peers):
+        vec_copy(vb, svb, rvb, i, dev, dev).wait_recv()
     tot = (vb[0] + vb[1]) + (vb[2] + vb[3])
     for i in range(2):
         vo[4 + i] = tot[i:i + 1]
     emit(vo, vec_hbm)
-
-    for g in (gat_h, gat_m, gat_g, gat_a):
-        g.drain()
-    for s in (sc_a, sc_g, sc_y, sc_h):
-        s.drain()
     for i, dev in enumerate(peers):
-        vec_copy(va, sva, rva, i, me, dev).wait_send()
         vec_copy(vb, svb, rvb, i, me, dev).wait_send()
     for c in outs:
         c.wait()
+    assert max(count.values()) <= NSEM
 
 
 GR = 320
@@ -409,6 +452,7 @@
         cr.start()
         loads.append((cl, cr))
     passes = [(y_in, yv, y_out), (gx_in, gxv, gx_out), (gbu_in, gv, gbu_out)]
+    srcs = (yv, gxv, gv.at[0])
     pin = [pltpu.make_async_copy(a, b, psem.at[i]) for i, (a, b, _) in enumerate(passes)]
     pin.append(pltpu.make_async_copy(vec_in, vv, psem.at[3]))
     for c in pin:
@@ -421,10 +465,10 @@
         dst = douts[i]
 
         def body(m, carry, off=off, r=r, dst=dst, step=step):
-            slot = lax.rem(m + step, 3)
+            slot = lax.rem(m + step, 4)
             out = pltpu.make_async_copy(st.at[slot], dst.at[pl.ds(pl.multiple_of(m * GR, GR), GR)], ssem.at[slot])
 
-            @pl.when(m + step >= 3)
+            @pl.when(m + step >= 4)
             def _():
                 out.wait()
             st[slot] = dot(lv[pl.ds(pl.multiple_of(off + m * GR, 64), GR), :], rv[r], NN).astype(BF16)
@@ -435,10 +479,10 @@
     for c in pin:
         c.wait()
     done = []
-    for i, (_, b, o) in enumerate(passes):
-        done.append(pltpu.make_async_copy(b, o, osem.at[i]))
+    for i, (_, _, o) in enumerate(passes):
+        done.append(pltpu.make_async_copy(srcs[i], o, osem.at[i]))
     for i, o in enumerate((v0, v1, v2, v3, v4, v5)):
-        done.append(pltpu.make_async_copy(vv.at[i], o, osem.at[3 + i]))
+        done.append(pltpu.make_async_copy(vv.at[i, 0], o, osem.at[3 + i]))
     ones = jnp.ones((16, SEQ), BF16)
     for h in range(NH):
         for t in range(3):
@@ -447,7 +491,7 @@
     done.append(pltpu.make_async_copy(gbq, gbq_hbm, osem.at[9]))
     for c in done:
         c.start()
-    for i in range(3):
+    for i in range(4):
         pltpu.make_async_copy(st.at[i], dwo.at[pl.ds(0, GR)], ssem.at[i]).wait()
     for c in done:
         c.wait()
@@ -455,7 +499,6 @@
 
 def solution(mesh):
     def local_step(x, ln1_gamma, ln1_beta, w_qkv, b_qkv, w_out, b_out, ln2_gamma, ln2_beta, w_up, b_up, w_down, b_down, grad_y):
-        row = lambda v: v.reshape(1, -1)
         wqt = jnp.transpose(w_qkv, (1, 2, 3, 0)).reshape(QKV, D)
         any_spec = pl.BlockSpec(memory_space=pl.ANY)
         sds = jax.ShapeDtypeStruct
@@ -468,46 +511,45 @@
             out_specs=(any_spec,) * 6,
             scratch_shapes=[
                 pltpu.VMEM((QKV, D), BF16), pltpu.VMEM((CTX, D), BF16), pltpu.VMEM((D, FF), BF16), pltpu.VMEM((FF, D), BF16),
-                pltpu.VMEM((ROWS, D), BF16), pltpu.VMEM((ROWS, D), BF16),
-                pltpu.VMEM((1, D), F32), pltpu.VMEM((1, D), F32), pltpu.VMEM((1, QKV), F32), pltpu.VMEM((1, D), F32),
-                pltpu.VMEM((1, D), F32), pltpu.VMEM((1, D), F32), pltpu.VMEM((1, FF), F32), pltpu.VMEM((1, D), F32),
+                pltpu.VMEM((2, ROWS, D), BF16),
+                pltpu.VMEM((1, D), F32), pltpu.VMEM((1, D), F32), pltpu.VMEM((3, NH, HD), F32), pltpu.VMEM((1, QKV), F32),
+                pltpu.VMEM((1, D), F32), pltpu.VMEM((1, D), F32), pltpu.VMEM((1, D), F32), pltpu.VMEM((1, FF), F32), pltpu.VMEM((1, D), F32),
                 pltpu.VMEM((4, SEQ, D), BF16), pltpu.VMEM((LROWS, SEQ), BF16), pltpu.VMEM((SEQ, D), BF16),
                 pltpu.VMEM((QKV, SEQ), BF16), pltpu.VMEM((SEQ, QKV), BF16), pltpu.VMEM((SEQ, CTX), BF16),
                 pltpu.VMEM((CTX, SEQ), BF16), pltpu.VMEM((NH, SEQ, SEQ), F32),
                 pltpu.VMEM((SEQ, FF), BF16), pltpu.VMEM((SEQ, FF), BF16),
-                pltpu.VMEM((ROWS, D), F32), pltpu.VMEM((ROWS, D), F32), pltpu.VMEM((2, ROWS, D), BF16),
+                pltpu.VMEM((2, ROWS, D), F32), pltpu.VMEM((ROWS, D), F32), pltpu.VMEM((2, ROWS, D), BF16),
                 pltpu.VMEM((1, FF), F32),
                 pltpu.VMEM((TP, 4, D), F32), pltpu.VMEM((TP, 2, D), F32), pltpu.VMEM((6, 1, D), F32),
                 pltpu.VMEM((4, 2, 2, ROWS, D), BF16), pltpu.VMEM((4, 2, ROWS, D), BF16),
-                pltpu.VMEM((4, ROWS, D), BF16), pltpu.VMEM((4, ROWS, D), BF16),
-                pltpu.SemaphoreType.DMA((4,)), pltpu.SemaphoreType.DMA((11,)), pltpu.SemaphoreType.DMA((10,)),
-                pltpu.SemaphoreType.DMA((82,)), pltpu.SemaphoreType.DMA((82,)),
+                pltpu.VMEM((4, 2, ROWS, D), BF16), pltpu.VMEM((4, 2, ROWS, D), BF16),
+                pltpu.SemaphoreType.DMA((4,)), pltpu.SemaphoreType.DMA((10,)), pltpu.SemaphoreType.DMA((9,)),
+                pltpu.SemaphoreType.DMA((NSEM,)), pltpu.SemaphoreType.DMA((NSEM,)),
             ],
             compiler_params=pltpu.CompilerParams(collective_id=0, has_side_effects=True, vmem_limit_bytes=66_000_000),
             cost_estimate=pl.CostEstimate(flops=10_000_000_000, bytes_accessed=45_000_000, transcendentals=1_000_000),
-        )(x[0], grad_y[0], wqt, w_out, w_up, w_down, row(ln1_gamma), row(ln1_beta), b_qkv.reshape(1, QKV), row(b_out),
-          row(ln2_gamma), row(ln2_beta), row(b_up), row(b_down))
+        )(x[0], grad_y[0], wqt, w_out, w_up, w_down, ln1_gamma, ln1_beta, jnp.transpose(b_qkv, (1, 0, 2)), b_out,
+          ln2_gamma, ln2_beta, b_up, b_down)
         y, gx, v0, v1, v2, v3, v4, v5, gbq, gbu, dwq, dwo, dwu, dwd = pl.pallas_call(
             grad_kernel,
             name='weight_grads',
-            out_shape=(sds((ROWS, D), BF16), sds((ROWS, D), BF16)) + (sds((1, D), F32),) * 6 + (
-                sds((3, NH, HD), F32), sds((1, FF), F32), sds((QKV, D), BF16), sds((CTX, D), BF16), sds((D, FF), BF16), sds((FF, D), BF16)),
+            out_shape=(sds((ROWS, D), BF16), sds((ROWS, D), BF16)) + (sds((D,), F32),) * 6 + (
+                sds((3, NH, HD), F32), sds((FF,), F32), sds((QKV, D), BF16), sds((CTX, D), BF16), sds((D, FF), BF16), sds((FF, D), BF16)),
             in_specs=[any_spec] * 6,
             out_specs=(any_spec,) * 14,
             scratch_shapes=[
-                pltpu.VMEM((LROWS, SEQ), BF16), pltpu.VMEM((4, SEQ, D), BF16), pltpu.VMEM((3, GR, D), BF16),
+                pltpu.VMEM((LROWS, SEQ), BF16), pltpu.VMEM((4, SEQ, D), BF16), pltpu.VMEM((4, GR, D), BF16),
                 pltpu.VMEM((ROWS, D), BF16), pltpu.VMEM((ROWS, D), BF16), pltpu.VMEM((6, 1, D), F32), pltpu.VMEM((1, FF), F32),
                 pltpu.VMEM((3, NH, HD), F32),
-                pltpu.SemaphoreType.DMA((8,)), pltpu.SemaphoreType.DMA((3,)), pltpu.SemaphoreType.DMA((4,)), pltpu.SemaphoreType.DMA((10,)),
+                pltpu.SemaphoreType.DMA((8,)), pltpu.SemaphoreType.DMA((4,)), pltpu.SemaphoreType.DMA((4,)), pltpu.SemaphoreType.DMA((10,)),
             ],
-            compiler_params=pltpu.CompilerParams(vmem_limit_bytes=40_000_000),
+            compiler_params=pltpu.CompilerParams(vmem_limit_bytes=66_000_000),
             cost_estimate=pl.CostEstimate(flops=5_000_000_000, bytes_accessed=44_000_000, transcendentals=0),
         )(y, gx, vec, gbu, lmat, rmat)
         g_wqkv = jnp.transpose(dwq.reshape(NH, 3, HD, D), (3, 0, 1, 2))
-        vecs = [v.reshape(D) for v in (v0, v1, v2, v3, v4, v5)]
-        g_ln2g, g_ln2b, g_bo, g_bd, g_ln1g, g_ln1b = vecs
+        g_ln2g, g_ln2b, g_bo, g_bd, g_ln1g, g_ln1b = v0, v1, v2, v3, v4, v5
         return (y[None], gx[None], g_ln1g, g_ln1b, g_wqkv, jnp.transpose(gbq, (1, 0, 2)), dwo, g_bo,
-                g_ln2g, g_ln2b, dwu, gbu.reshape(FF), dwd, g_bd)
+                g_ln2g, g_ln2b, dwu, gbu, dwd, g_bd)
 
     row_spec = P('dp', 'tp', None)
     in_specs = (row_spec, P(), P(), P(None, 'tp', None, None), P('tp', None, None), P('tp', None), P(), P(), P(),

time: 110 us -> 78.6 us (0.71)
  local copies, waits for them, and re-layouts: 17.2 us -> 0 us
  Pallas kernels: 86.6 us -> 77.8 us
  other arithmetic: 4.39 us -> 0 us
    reshape x8 -> x0, local copies, waits for them, and re-layouts: 9.87 us -> none  [the longest x7 9.19 us: local_step(): row = lambda v: v.reshape(1, -1)]
    pallas_call x1, Pallas kernels: 68.9 us -> 61.3 us  [local_step(): pl.pallas_call(block_kernel, name='block', out_shape=(sds((ROWS, D), BF16...]
    unnamed x13 -> x0, local copies, waits for them, and re-layouts: 7.35 us -> none
    pallas_call x7 -> x0, other arithmetic: 4.39 us -> none  [local_step(): pl.pallas_call(grad_kernel, name='weight_grads', out_shape=(sds((ROWS, D)...]
    pallas_call x1, Pallas kernels: 17.7 us -> 16.5 us  [local_step(): pl.pallas_call(grad_kernel, name='weight_grads', out_shape=(sds((ROWS, D)...]
where the time goes in v2:
time: 78.6 us; the launch traced here: 78.5 us
  Pallas kernels  77.8 us (99%)
    pallas_call x1, Pallas kernels, local_step(): pl.pallas_call(block_kernel, name='block', out_shape=(sds((ROWS, D), BF16...  61.3 us
    pallas_call x1, Pallas kernels, local_step(): pl.pallas_call(grad_kernel, name='weight_grads', out_shape=(sds((ROWS, D)...  16.5 us

profile of v2, /device:TPU:0, one launch (start us, length us, event | category | flops | bytes accessed | tf_op | source)
XLA Modules:
  0.0 78.5 jit_solution(3746676537392722019)
XLA Ops:
  0.7 61.3 %block.1 = (bf16[32,2560]{1,0:T(8,128)(2,1)}, bf16[32,2560]{1,0:T(8,128)(2,1)}, f32[6,1,2560]{2,1,0:T(1,128)}, f32[1,2560]{1,0:T(1,128)}, bf16[7680,128]{1,0:T(8,128)(2,1)}, /*index=5*/bf16[4,128,2560]{2,1,0:T(8,128)(2,1)}) custom-call(bf16[32,2560]{1,0:T(8,128)(2,1)} %bitcast.13, bf16[32,2560]{1,0:T(8,128)(2,1)} %bitcast.14, bf16[1920,2560]{1,0:T(8,128)(2,1)} %bitcast.12, ...), custom_call_target="tpu_custom_call" | custom-call | flops 10000000000 | bytes 45000000 | tf_op jit(solution)/shard_map/block/pallas_call | solution.py:505
  62.0 16.5 %weight_grads.1 = (bf16[32,2560]{1,0:T(8,128)(2,1)}, bf16[32,2560]{1,0:T(8,128)(2,1)}, f32[2560]{0:T(1024)}, f32[2560]{0:T(1024)}, f32[2560]{0:T(1024)}, /*index...) custom-call(bf16[32,2560]{1,0:T(8,128)(2,1)} %get-tuple-element.34.y, ...), custom_call_target="tpu_custom_call" | custom-call | flops 5000000000 | bytes 44000000 | tf_op jit(solution)/shard_map/weight_grads/pallas_call | solution.py:533

commit v3 on v2

--- a/solution.py
+++ b/solution.py
@@ -196,23 +196,23 @@
                 self.sb[0, :, c] = (self.p[1 - ax, ak, :, c].astype(F32) + self.x1[1 - ax, :, c].astype(F32)).astype(BF16)
             self.over(n).start()
 
-        def run(self, fn, relay=True):
+        def run(self, fn, lag, also=None):
             def body(n, carry):
                 self.produce(n, fn(self.cols(n)))
-                if relay:
-                    @pl.when(n > 0)
+                if lag < RSC:
+                    @pl.when(n >= lag)
                     def _():
-                        self.relay(n - 1)
+                        self.relay(n - lag)
+                if also is not None:
+                    also(n)
                 return carry
             lax.fori_loop(0, RSC, body, 0)
-            if relay:
-                self.relay(RSC - 1)
-
-        def relay_all(self):
+
+        def relay_from(self, first):
             def body(n, carry):
                 self.relay(n)
                 return carry
-            lax.fori_loop(0, RSC, body, 0)
+            lax.fori_loop(first, RSC, body, 0)
 
         def arrive(self):
             for n in range(RSC):
@@ -263,7 +263,7 @@
         sh_h.finish(b, i)
     emit(rbuf.at[2], r_hbm.at[2])
 
-    QC = 384
+    QC = 640
 
     def qkv_body(n, carry):
         r0 = pl.multiple_of(n * QC, QC)
@@ -294,14 +294,15 @@
         ctx[:, t * 128:(t + 1) * 128] = lbuf[OFF_O + t * 128:OFF_O + (t + 1) * 128, :].T
 
     wcopies[1].wait()
-    sc_a.run(lambda cols: dot(ctx[...], wo[:, cols], NN))
+    sc_a.run(lambda cols: dot(ctx[...], wo[:, cols], NN), RSC)
+    sc_a.relay_from(0)
 
     for c in range(AGC):
         gat_m.forward(c)
     wcopies[2].wait()
     gat_m.finish()
     emit(rbuf.at[1], r_hbm.at[1])
-    FC = 256
+    FC = 512
 
     def dact_body(n, carry):
         f0 = pl.multiple_of(n * FC, FC)
@@ -319,7 +320,7 @@
     for b, i in blocks:
         sh_g.finish(b, i)
 
-    UC = 512
+    UC = 1280
     k0 = 0.7978845608028654
     k1 = 0.044715
 
@@ -342,18 +343,15 @@
 
     def dg_chunk(cols):
         return dot(rbuf[0], wu[cols, :], NT)
-    sc_g.run(dg_chunk)
-
-    sc_y.run(lambda cols: dot(act[...], wd[:, cols], NN))
-
-    def tr_body(src, off):
-        def body(n, carry):
-            r0 = pl.multiple_of(n * 128, 128)
-            lbuf[pl.ds(off + r0, 128), :] = src[:, pl.ds(r0, 128)].T
-            return carry
-        return body
-    lax.fori_loop(0, FF // 128, tr_body(act, OFF_ACT), 0)
-    lax.fori_loop(0, D // 128, tr_body(gbuf, OFF_G), 0)
+    sc_g.run(dg_chunk, 2)
+
+    def rest(n):
+        @pl.when(n < 2)
+        def _():
+            sc_g.relay(n + RSC - 2)
+    sc_y.run(lambda cols: dot(act[...], wd[:, cols], NN), RSC, rest)
+    sc_y.relay_from(0)
+
     va[me, 3:4, :] = jnp.sum(rbuf[1, rows(me), :].astype(F32), axis=0, keepdims=True)
 
     sc_g.arrive()
@@ -396,9 +394,10 @@
         lbuf[r0 + 2 * HD:r0 + 3 * HD, :] = dot(dot_h, p.astype(BF16), NT).astype(BF16)
     for t in range(QKV // 128):
         dqkv[:, t * 128:(t + 1) * 128] = lbuf[OFF_QKV + t * 128:OFF_QKV + (t + 1) * 128, :].T
-    emit(lbuf, l_hbm)
-
-    sc_h.run(lambda cols: dot(dqkv[...], wq[:, cols], NN))
+    emit(lbuf.at[pl.ds(OFF_QKV, QKV + CTX)], l_hbm.at[pl.ds(OFF_QKV, QKV + CTX)])
+
+    sc_h.run(lambda cols: dot(dqkv[...], wq[:, cols], NN), 3)
+    sc_h.relay_from(RSC - 3)
 
     sc_y.arrive()
     outb[0] = (x1[ax] + sc_y.own() + bd[...]).astype(BF16)
@@ -408,6 +407,16 @@
     tot = (va[0] + va[1]) + (va[2] + va[3])
     for i in range(4):
         vo[i] = tot[i:i + 1]
+
+    def tr_body(src, off):
+        def body(n, carry):
+            r0 = pl.multiple_of(n * 128, 128)
+            lbuf[pl.ds(off + r0, 128), :] = src[:, pl.ds(r0, 128)].T
+            return carry
+        return body
+    lax.fori_loop(0, FF // 128, tr_body(act, OFF_ACT), 0)
+    lax.fori_loop(0, D // 128, tr_body(gbuf, OFF_G), 0)
+    emit(lbuf.at[pl.ds(0, OFF_QKV)], l_hbm.at[pl.ds(0, OFF_QKV)])
 
     sc_h.arrive()
     dhl = sc_h.own()
@@ -438,14 +447,15 @@
     assert max(count.values()) <= NSEM
 
 
-GR = 320
-SECTIONS = ((OFF_ACT, FF, 1), (OFF_G, D, 0), (OFF_QKV, QKV, 2), (OFF_O, CTX, 3))
+SECTIONS = ((OFF_ACT, FF, 1, 640), (OFF_G, D, 0, 640), (OFF_QKV, QKV, 2, 640), (OFF_O, CTX, 3, 320))
+GR = 640
+SLOTS = 4
 
 
 def grad_kernel(y_in, gx_in, vec_in, gbu_in, l_hbm, r_hbm, y_out, gx_out, v0, v1, v2, v3, v4, v5, gbq_hbm, gbu_out,
                 dwq, dwo, dwu, dwd, lv, rv, st, yv, gxv, vv, gv, gbq, isem, ssem, psem, osem):
     loads = []
-    for i, (off, n, r) in enumerate(SECTIONS):
+    for i, (off, n, r, _) in enumerate(SECTIONS):
         cl = pltpu.make_async_copy(l_hbm.at[pl.ds(off, n)], lv.at[pl.ds(off, n)], isem.at[2 * i])
         cr = pltpu.make_async_copy(r_hbm.at[r], rv.at[r], isem.at[2 * i + 1])
         cl.start()
@@ -459,23 +469,27 @@
         c.start()
     douts = (dwd, dwu, dwq, dwo)
     step = 0
-    for i, (off, n, r) in enumerate(SECTIONS):
+    last = []
+
+    def out_copy(slot, dst, r0, gr):
+        return pltpu.make_async_copy(st.at[slot, pl.ds(0, gr)], dst.at[pl.ds(r0, gr)], ssem.at[slot])
+    for i, (off, n, r, gr) in enumerate(SECTIONS):
         loads[i][0].wait()
         loads[i][1].wait()
         dst = douts[i]
 
-        def body(m, carry, off=off, r=r, dst=dst, step=step):
-            slot = lax.rem(m + step, 4)
-            out = pltpu.make_async_copy(st.at[slot], dst.at[pl.ds(pl.multiple_of(m * GR, GR), GR)], ssem.at[slot])
-
-            @pl.when(m + step >= 4)
+        def body(m, carry, off=off, r=r, dst=dst, step=step, gr=gr):
+            slot = lax.rem(m + step, SLOTS)
+
+            @pl.when(m + step >= SLOTS)
             def _():
-                out.wait()
-            st[slot] = dot(lv[pl.ds(pl.multiple_of(off + m * GR, 64), GR), :], rv[r], NN).astype(BF16)
-            out.start()
+                out_copy(slot, dwd, 0, GR).wait()
+            st[slot, 0:gr] = dot(lv[pl.ds(pl.multiple_of(off + m * gr, 64), gr), :], rv[r], NN).astype(BF16)
+            out_copy(slot, dst, pl.multiple_of(m * gr, gr), gr).start()
             return carry
-        lax.fori_loop(0, n // GR, body, 0)
-        step += n // GR
+        lax.fori_loop(0, n // gr, body, 0)
+        last += [((step + m) % SLOTS, gr) for m in range(n // gr)]
+        step += n // gr
     for c in pin:
         c.wait()
     done = []
@@ -491,8 +505,8 @@
     done.append(pltpu.make_async_copy(gbq, gbq_hbm, osem.at[9]))
     for c in done:
         c.start()
-    for i in range(4):
-        pltpu.make_async_copy(st.at[i], dwo.at[pl.ds(0, GR)], ssem.at[i]).wait()
+    for slot, gr in last[-SLOTS:]:
+        out_copy(slot, dwo, 0, gr).wait()
     for c in done:
         c.wait()
 
@@ -523,7 +537,7 @@
                 pltpu.VMEM((TP, 4, D), F32), pltpu.VMEM((TP, 2, D), F32), pltpu.VMEM((6, 1, D), F32),
                 pltpu.VMEM((4, 2, 2, ROWS, D), BF16), pltpu.VMEM((4, 2, ROWS, D), BF16),
                 pltpu.VMEM((4, 2, ROWS, D), BF16), pltpu.VMEM((4, 2, ROWS, D), BF16),
-                pltpu.SemaphoreType.DMA((4,)), pltpu.SemaphoreType.DMA((10,)), pltpu.SemaphoreType.DMA((9,)),
+                pltpu.SemaphoreType.DMA((4,)), pltpu.SemaphoreType.DMA((10,)), pltpu.SemaphoreType.DMA((10,)),
                 pltpu.SemaphoreType.DMA((NSEM,)), pltpu.SemaphoreType.DMA((NSEM,)),
             ],
             compiler_params=pltpu.CompilerParams(collective_id=0, has_side_effects=True, vmem_limit_bytes=66_000_000),
@@ -538,7 +552,7 @@
             in_specs=[any_spec] * 6,
             out_specs=(any_spec,) * 14,
             scratch_shapes=[
-                pltpu.VMEM((LROWS, SEQ), BF16), pltpu.VMEM((4, SEQ, D), BF16), pltpu.VMEM((4, GR, D), BF16),
+                pltpu.VMEM((LROWS, SEQ), BF16), pltpu.VMEM((4, SEQ, D), BF16), pltpu.VMEM((SLOTS, GR, D), BF16),
                 pltpu.VMEM((ROWS, D), BF16), pltpu.VMEM((ROWS, D), BF16), pltpu.VMEM((6, 1, D), F32), pltpu.VMEM((1, FF), F32),
                 pltpu.VMEM((3, NH, HD), F32),
                 pltpu.SemaphoreType.DMA((8,)), pltpu.SemaphoreType.DMA((4,)), pltpu.SemaphoreType.DMA((4,)), pltpu.SemaphoreType.DMA((10,)),

time: 78.6 us -> 74.9 us (0.953)
  Pallas kernels: 77.8 us -> 74.2 us
    pallas_call x1, Pallas kernels: 61.3 us -> 58.9 us  [local_step(): pl.pallas_call(block_kernel, name='block', out_shape=(sds((ROWS, D), BF16...]
    pallas_call x1, Pallas kernels: 16.5 us -> 15.3 us  [local_step(): pl.pallas_call(grad_kernel, name='weight_grads', out_shape=(sds((ROWS, D)...]
where the time goes in v3:
time: 74.9 us; the launch traced here: 74.8 us
  Pallas kernels  74.2 us (99%)
    pallas_call x1, Pallas kernels, local_step(): pl.pallas_call(block_kernel, name='block', out_shape=(sds((ROWS, D), BF16...  58.9 us
    pallas_call x1, Pallas kernels, local_step(): pl.pallas_call(grad_kernel, name='weight_grads', out_shape=(sds((ROWS, D)...  15.3 us

profile of v3, /device:TPU:0, one launch (start us, length us, event | category | flops | bytes accessed | tf_op | source)
XLA Modules:
  0.0 74.8 jit_solution(10450330126286127837)
XLA Ops:
  0.7 58.9 %block.1 = (bf16[32,2560]{1,0:T(8,128)(2,1)}, bf16[32,2560]{1,0:T(8,128)(2,1)}, f32[6,1,2560]{2,1,0:T(1,128)}, f32[1,2560]{1,0:T(1,128)}, bf16[7680,128]{1,0:T(8,128)(2,1)}, /*index=5*/bf16[4,128,2560]{2,1,0:T(8,128)(2,1)}) custom-call(bf16[32,2560]{1,0:T(8,128)(2,1)} %bitcast.13, bf16[32,2560]{1,0:T(8,128)(2,1)} %bitcast.14, bf16[1920,2560]{1,0:T(8,128)(2,1)} %bitcast.12, ...), custom_call_target="tpu_custom_call" | custom-call | flops 10000000000 | bytes 45000000 | tf_op jit(solution)/shard_map/block/pallas_call | solution.py:519
  59.6 15.3 %weight_grads.1 = (bf16[32,2560]{1,0:T(8,128)(2,1)}, bf16[32,2560]{1,0:T(8,128)(2,1)}, f32[2560]{0:T(1024)}, f32[2560]{0:T(1024)}, f32[2560]{0:T(1024)}, /*index...) custom-call(bf16[32,2560]{1,0:T(8,128)(2,1)} %get-tuple-element.34.y, ...), custom_call_target="tpu_custom_call" | custom-call | flops 5000000000 | bytes 44000000 | tf_op jit(solution)/shard_map/weight_grads/pallas_call | solution.py:547
